TPU v7x, 128 devices: a whole 4x4x4 slice. The times are simulated.
128 devices in a mesh: cp: 32 (over x, y, core), tp: 4 (over z).
Axes of the slice: x: 4, y: 4, z: 4, core: 2. Of those that a mesh axis runs over, the one named last changes fastest.
Arguments:
- hidden: bfloat16 [8192, 4096], P('cp', 'tp'), may hold values from -120 to 120
- query_weight: bfloat16 [4096, 4096], P(None, 'tp'), may hold values from -0.1875 to 0.1875
- key_matrix: bfloat16 [4096, 512], P(None, 'tp'), may hold values from -0.09375 to 0.09375
- value_matrix: bfloat16 [4096, 512], P(None, 'tp'), may hold values from -0.09375 to 0.09375
- output_weight: bfloat16 [4096, 4096], P('tp'), may hold values from -0.1875 to 0.1875
- document_bounds: int32 [9], replicated, may hold values from 0 to 8192, as said below
- block_owner: int32 [64], replicated, may hold values from 0 to 31, as said below
Outputs:
- attended: bfloat16 [8192, 4096], P('cp', 'tp')
Inputs may be any that keep to these rules, and one draw needn't show every extreme that they name: document_bounds[0] = 0, document_bounds[8] = 8192, strictly rising; document i holds the tokens from document_bounds[i] to document_bounds[i + 1] - 1. `block_owner`: every index of cp is named by exactly 2 blocks.
All inputs are finite; a program needn't handle non-finite values.
Results may differ from a plain program's by a relative error of at most 0.012.
The roundings to bfloat16 on the way count: a program that leaves them out, or rounds other values in their place, can miss the bound.
Values may be sent and summed in bfloat16 or wider, within the bound.
A program may use at most 128 MiB of HBM per device.

v0:
```python
import functools
import math

import jax
import jax.numpy as jnp
from jax import lax
from jax.experimental import pallas as pl
from jax.experimental.pallas import tpu as pltpu
from jax.sharding import PartitionSpec as P

HEAD = 128
BLOCK = 128
CP = 32
TP = 4
ROWS = 256
WIDTH = 1024
NBLK = 64
HEADS = 8
TOKENS = 8192
PORTION = BLOCK // CP

rope_theta = 500000.0
rope_factor = 8.0
rope_context = 8192.0
masked_score = -1e30
MESH = pl.DeviceIdType.MESH


def rope_inverse(head_size):
    halves = jnp.arange(head_size // 2, dtype=jnp.float32)
    inverse = 1.0 / rope_theta ** (2.0 * halves / head_size)
    wavelength = 2.0 * math.pi / inverse
    smooth = (rope_context / wavelength - 1.0) / 3.0
    blended = (1.0 - smooth) * inverse / rope_factor + smooth * inverse
    longer = jnp.where(wavelength > rope_context, inverse / rope_factor, blended)
    return jnp.where(wavelength < rope_context / 4.0, inverse, longer)


def slots_of(block_owner):
    blocks = jnp.arange(NBLK, dtype=jnp.int32)
    same = block_owner[:, None] == block_owner[None, :]
    earlier = blocks[None, :] < blocks[:, None]
    rank = jnp.sum((same & earlier).astype(jnp.int32), axis=1)
    return block_owner * 2 + rank


def starts_of(tokens, bounds_ref):
    start = jnp.zeros_like(tokens)
    for i in range(1, 8):
        bound = bounds_ref[i]
        start = jnp.where(tokens >= bound, bound, start)
    return start


def gather_kernel(
    bounds_ref, hidden_ref, wq_ref, wk_ref, wv_ref, inverse_ref,
    k_ref, v_ref, q_ref,
    full, wq, wkv, qtmp, qsend, cosine, sine,
    w_sem, z_send, z_recv, g_send, g_recv, q_send, q_recv,
):
    me = lax.axis_index("cp")
    tp = lax.axis_index("tp")
    core = lax.rem(me, 2)
    ycoord = lax.rem(me // 2, 4)
    xcoord = me // 8
    partner = me + 1 - 2 * core
    up, down = lax.rem(tp + 1, TP), lax.rem(tp + 3, TP)

    weights = [
        pltpu.make_async_copy(wk_ref, wkv.at[:, pl.ds(0, HEAD)], w_sem.at[0]),
        pltpu.make_async_copy(wv_ref, wkv.at[:, pl.ds(HEAD, HEAD)], w_sem.at[1]),
        pltpu.make_async_copy(wq_ref, wq, w_sem.at[2]),
    ]
    for copy in weights:
        copy.start()

    barrier = pltpu.get_barrier_semaphore()

    def greet(k, carry):
        pl.semaphore_signal(
            barrier, inc=1, device_id={"cp": lax.rem(me + k, CP)}, device_id_type=MESH
        )
        return carry

    pl.semaphore_signal(barrier, inc=1, device_id={"tp": up}, device_id_type=MESH)
    pl.semaphore_signal(barrier, inc=1, device_id={"tp": down}, device_id_type=MESH)
    lax.fori_loop(1, CP, greet, 0)
    pl.semaphore_wait(barrier, CP + 1)

    def zcopy(n, source, target, owner, row, count):
        columns = pl.ds(pl.multiple_of(owner * WIDTH, WIDTH), WIDTH)
        source_ref = (
            hidden_ref.at[pl.ds(row, count), :]
            if source
            else full.at[pl.ds(row, count), columns]
        )
        return pltpu.make_async_remote_copy(
            src_ref=source_ref,
            dst_ref=full.at[pl.ds(row, count), columns],
            send_sem=z_send.at[n],
            recv_sem=z_recv.at[n],
            device_id={"tp": target},
            device_id_type=MESH,
        )

    own = {}
    for n, (row, count) in enumerate(((0, 128), (128, 64), (192, 64))):
        own[n] = (
            zcopy(2 * n, True, up, tp, row, count),
            zcopy(2 * n + 1, True, down, tp, row, count),
        )
    fwd = {
        r: (
            zcopy(6 + 2 * r, False, up, down, r * 128, 64),
            zcopy(7 + 2 * r, False, down, up, r * 128 + 64, 64),
        )
        for r in range(2)
    }
    for n in (0, 1):
        for copy in own[n]:
            copy.start()

    full[:, pl.ds(pl.multiple_of(tp * WIDTH, WIDTH), WIDTH)] = hidden_ref[...]
    inverse = inverse_ref[...]
    lanes = lax.broadcasted_iota(jnp.int32, (BLOCK, HEAD), 1)
    for r in range(2):
        tokens = me * ROWS + r * BLOCK + lax.broadcasted_iota(jnp.int32, (BLOCK, HEAD), 0)
        angle = (tokens - starts_of(tokens, bounds_ref)).astype(jnp.float32) * inverse
        turn = jnp.sin(angle)
        cosine[pl.ds(r * BLOCK, BLOCK), :] = jnp.cos(angle)
        sine[pl.ds(r * BLOCK, BLOCK), :] = jnp.where(lanes < HEAD // 2, -turn, turn)
    weights[0].wait()
    weights[1].wait()

    for copy in own[0]:
        copy.wait_recv()
    for copy in fwd[0]:
        copy.start()
    for copy in own[2]:
        copy.start()
    weights[2].wait()

    def rotate(raw, r):
        table = pl.ds(r * BLOCK, BLOCK)
        return raw * cosine[table, :] + pltpu.roll(raw, HEAD // 2, 1) * sine[table, :]

    def keys_values(r):
        raw = jnp.dot(
            full[pl.ds(r * BLOCK, BLOCK), :], wkv[...], preferred_element_type=jnp.float32
        )
        k_ref[xcoord, ycoord, core, r] = rotate(raw[:, :HEAD], r).astype(jnp.bfloat16)
        v_ref[xcoord, ycoord, core, r] = raw[:, HEAD:].astype(jnp.bfloat16)

    def queries(r):
        def pair(n, carry):
            columns = pl.ds(pl.multiple_of(n * 2 * HEAD, 2 * HEAD), 2 * HEAD)
            raw = jnp.dot(
                full[pl.ds(r * BLOCK, BLOCK), :],
                wq[:, columns],
                preferred_element_type=jnp.float32,
            )
            turned = jnp.concatenate(
                [rotate(raw[:, :HEAD], r), rotate(raw[:, HEAD:], r)], axis=1
            )
            qtmp[pl.ds(r * BLOCK, BLOCK), columns] = turned.astype(jnp.bfloat16)
            return carry

        lax.fori_loop(0, WIDTH // (2 * HEAD), pair, 0)

    def gather(which, r):
        buffer = (k_ref, v_ref)[which]
        a, b = ((xcoord, ycoord), (ycoord, xcoord))[which]
        base = (which * 2 + r) * 12

        def neighbour(along, step):
            if along == 0:
                na, nb = lax.rem(a + step, 4), b
            else:
                na, nb = a, lax.rem(b + step, 4)
            x, y = ((na, nb), (nb, na))[which]
            return (x * 4 + y) * 2 + core

        def copy(n, ref, target):
            return pltpu.make_async_remote_copy(
                src_ref=ref,
                dst_ref=ref,
                send_sem=g_send.at[base + n],
                recv_sem=g_recv.at[base + n],
                device_id={"cp": target},
                device_id_type=MESH,
            )

        def piece(at, row, count):
            rows = pl.ds(row, count)
            if which == 0:
                return buffer.at[at, b, core, r, rows]
            return buffer.at[b, at, core, r, rows]

        def line(at, first, count):
            along = pl.ds(first, count)
            if which == 0:
                return buffer.at[along, at, core, r]
            return buffer.at[at, along, core, r]

        a_next, a_prev = lax.rem(a + 1, 4), lax.rem(a + 3, 4)
        b_next, b_prev = lax.rem(b + 1, 4), lax.rem(b + 3, 4)
        b_far = lax.rem(b + 2, 4)
        return dict(
            ring1=(
                copy(0, piece(a, 0, BLOCK), neighbour(0, 1)),
                copy(1, piece(a, 0, BLOCK), neighbour(0, 3)),
            ),
            ring1_far=(
                copy(2, piece(a_prev, 0, 64), neighbour(0, 1)),
                copy(3, piece(a_next, 64, 64), neighbour(0, 3)),
            ),
            ring2=(
                copy(4, line(b, 0, 4), neighbour(1, 1)),
                copy(5, line(b, 0, 4), neighbour(1, 3)),
            ),
            ring2_far=(
                copy(6, line(b_prev, 0, 2), neighbour(1, 1)),
                copy(7, line(b_next, 2, 2), neighbour(1, 3)),
            ),
            across=(
                copy(8, line(b, 0, 4), partner),
                copy(9, line(b_prev, 0, 4), partner),
                copy(10, line(b_next, 0, 4), partner),
                copy(11, line(b_far, 0, 4), partner),
            ),
        )

    flows = {r: [gather(which, r) for which in range(2)] for r in range(2)}

    def start(r, name):
        for flow in flows[r]:
            for copy in flow[name]:
                copy.start()

    def arrived(r, name):
        for flow in flows[r]:
            for copy in flow[name]:
                copy.wait_recv()

    def across(r, which):
        for flow in flows[r]:
            for n in which:
                flow["across"][n].start()

    for copy in fwd[0]:
        copy.wait_recv()
    keys_values(0)
    start(0, "ring1")
    for n in (1, 2):
        for copy in own[n]:
            copy.wait_recv()
    for copy in fwd[1]:
        copy.start()
    queries(0)
    arrived(0, "ring1")
    start(0, "ring1_far")
    arrived(0, "ring1_far")
    start(0, "ring2")
    across(0, (0,))
    for copy in fwd[1]:
        copy.wait_recv()
    keys_values(1)
    start(1, "ring1")
    arrived(0, "ring2")
    start(0, "ring2_far")
    across(0, (1, 2))
    queries(1)
    arrived(1, "ring1")
    start(1, "ring1_far")

    out_row = lax.broadcasted_iota(jnp.int32, (ROWS, ROWS), 0)
    in_row = lax.broadcasted_iota(jnp.int32, (ROWS, ROWS), 1)
    origin = lax.rem(out_row // 4, 2) * BLOCK + (out_row // 8) * 4 + lax.rem(out_row, 4)
    pick = (in_row == origin).astype(jnp.float32).astype(jnp.bfloat16)
    ordered = jnp.dot(pick, qtmp[...], preferred_element_type=jnp.float32)
    qsend[...] = ordered.reshape(CP, 8, WIDTH).astype(jnp.bfloat16)
    q_ref[me] = qsend[me]

    def qcopy(k, target, slot):
        return pltpu.make_async_remote_copy(
            src_ref=qsend.at[target],
            dst_ref=q_ref.at[slot],
            send_sem=q_send.at[k],
            recv_sem=q_recv.at[k],
            device_id={"cp": target},
            device_id_type=MESH,
        )

    def send_queries(k, carry):
        qcopy(k, lax.rem(me + k, CP), me).start()
        return carry

    def wait_queries(k, carry):
        copy = qcopy(k, lax.rem(me + k, CP), lax.rem(me + CP - k, CP))
        copy.wait_send()
        copy.wait_recv()
        return carry

    arrived(1, "ring1_far")
    start(1, "ring2")
    across(1, (0,))
    lax.fori_loop(1, CP, send_queries, 0)
    arrived(0, "ring2_far")
    across(0, (3,))
    arrived(1, "ring2")
    start(1, "ring2_far")
    across(1, (1, 2))
    arrived(1, "ring2_far")
    across(1, (3,))
    lax.fori_loop(1, CP, wait_queries, 0)
    for r in range(2):
        arrived(r, "across")
        for flow in flows[r]:
            for name in ("ring1", "ring1_far", "ring2", "ring2_far", "across"):
                for copy in flow[name]:
                    copy.wait_send()
    for group in (*own.values(), *fwd.values()):
        for copy in group:
            copy.wait_send()


def gather_call(bounds, hidden, wq, wk, wv, inverse):
    vmem = pl.BlockSpec(memory_space=pltpu.VMEM)
    anywhere = pl.BlockSpec(memory_space=pl.ANY)
    kv = jax.ShapeDtypeStruct((4, 4, 2, 2, BLOCK, HEAD), jnp.bfloat16)
    dma = pltpu.SemaphoreType.DMA
    return pl.pallas_call(
        gather_kernel,
        out_shape=(kv, kv, jax.ShapeDtypeStruct((CP, 8, WIDTH), jnp.bfloat16)),
        in_specs=[
            pl.BlockSpec(memory_space=pltpu.SMEM), vmem, anywhere, anywhere, anywhere, vmem,
        ],
        out_specs=(vmem, vmem, vmem),
        scratch_shapes=[
            pltpu.VMEM((ROWS, TP * WIDTH), jnp.bfloat16),
            pltpu.VMEM((TP * WIDTH, WIDTH), jnp.bfloat16),
            pltpu.VMEM((TP * WIDTH, 2 * HEAD), jnp.bfloat16),
            pltpu.VMEM((ROWS, WIDTH), jnp.bfloat16),
            pltpu.VMEM((CP, 8, WIDTH), jnp.bfloat16),
            pltpu.VMEM((ROWS, HEAD), jnp.float32),
            pltpu.VMEM((ROWS, HEAD), jnp.float32),
            dma((3,)), dma((10,)), dma((10,)), dma((48,)), dma((48,)), dma((CP,)), dma((CP,)),
        ],
        compiler_params=pltpu.CompilerParams(
            collective_id=0, has_side_effects=True, vmem_limit_bytes=50 * 1024 * 1024
        ),
        name="gather_project",
    )(bounds, hidden, wq, wk, wv, inverse)


GROUP = 8
TILE = 512


def attend_kernel(bounds_ref, q_ref, k_ref, v_ref, o_ref):
    me = lax.axis_index("cp")
    rows = GROUP * PORTION
    scale = 1.0 / math.sqrt(HEAD)

    def group(g, carry):
        first = pl.multiple_of(g * rows, rows)
        q = jnp.concatenate(
            [q_ref[pl.ds(first, rows), h * HEAD : (h + 1) * HEAD] for h in range(HEADS)], axis=0
        )
        row = lax.rem(lax.broadcasted_iota(jnp.int32, (HEADS * rows, 1), 0), rows)
        tokens = (g * GROUP + row // PORTION) * BLOCK + me * PORTION + lax.rem(row, PORTION)
        starts = starts_of(tokens, bounds_ref)
        low_token = g * GROUP * BLOCK
        low = jnp.int32(0)
        for i in range(1, 8):
            low = jnp.where(low_token >= bounds_ref[i], bounds_ref[i], low)

        def tile(j, state):
            top, total, mixed = state
            at = pl.ds(pl.multiple_of(j * TILE, TILE), TILE)
            scores = lax.dot_general(
                q, k_ref[at, :], (((1,), (1,)), ((), ())), preferred_element_type=jnp.float32
            )
            keys = j * TILE + lax.broadcasted_iota(jnp.int32, (HEADS * rows, TILE), 1)
            allowed = (keys >= starts) & (keys <= tokens)
            scores = jnp.where(allowed, scores * scale, masked_score)
            new_top = jnp.maximum(top, jnp.max(scores, axis=1, keepdims=True))
            weights = jnp.where(allowed, jnp.exp(scores - new_top), 0.0)
            factor = jnp.exp(top - new_top)
            part = weights[:, :HEAD]
            for c in range(1, TILE // HEAD):
                part = part + weights[:, c * HEAD : (c + 1) * HEAD]
            total = total * factor + part
            mixed = mixed * factor + jnp.dot(
                weights.astype(jnp.bfloat16), v_ref[at, :], preferred_element_type=jnp.float32
            )
            return new_top, total, mixed

        top, total, mixed = lax.fori_loop(
            low // TILE,
            (g + 1) * (GROUP * BLOCK // TILE),
            tile,
            (
                jnp.full((HEADS * rows, 1), masked_score, jnp.float32),
                jnp.zeros((HEADS * rows, HEAD), jnp.float32),
                jnp.zeros((HEADS * rows, HEAD), jnp.float32),
            ),
        )
        out = (mixed / jnp.sum(total, axis=1, keepdims=True)).astype(jnp.bfloat16)
        for h in range(HEADS):
            o_ref[pl.ds(first, rows), h * HEAD : (h + 1) * HEAD] = out[h * rows : (h + 1) * rows]
        return carry

    lax.fori_loop(0, NBLK // GROUP, group, 0)


def attend_call(bounds, q, k, v):
    vmem = pl.BlockSpec(memory_space=pltpu.VMEM)
    return pl.pallas_call(
        attend_kernel,
        out_shape=jax.ShapeDtypeStruct((ROWS, WIDTH), jnp.bfloat16),
        in_specs=[pl.BlockSpec(memory_space=pltpu.SMEM), vmem, vmem, vmem],
        out_specs=vmem,
        compiler_params=pltpu.CompilerParams(vmem_limit_bytes=40 * 1024 * 1024),
        name="attend",
    )(bounds, q, k, v)


CHUNKS = 4
CW = WIDTH // CHUNKS


def output_kernel(
    slot_ref, heads_ref, wo_ref, out_ref,
    wo, far, near, far_in, near_in, spread, landed, own_sum,
    w_sem, z_send, z_recv, a_send, a_recv,
):
    me = lax.axis_index("cp")
    tp = lax.axis_index("tp")
    up, down, across = lax.rem(tp + 1, TP), lax.rem(tp + 3, TP), lax.rem(tp + 2, TP)

    loads = []
    for n, t in enumerate((across, up, down, tp)):
        columns = pl.ds(pl.multiple_of(t * WIDTH, WIDTH), WIDTH)
        loads.append(pltpu.make_async_copy(wo_ref.at[:, columns], wo.at[n], w_sem.at[n]))
        loads[-1].start()

    barrier = pltpu.get_barrier_semaphore()

    def greet(k, carry):
        pl.semaphore_signal(
            barrier, inc=1, device_id={"cp": lax.rem(me + k, CP)}, device_id_type=MESH
        )
        return carry

    pl.semaphore_signal(barrier, inc=1, device_id={"tp": up}, device_id_type=MESH)
    pl.semaphore_signal(barrier, inc=1, device_id={"tp": down}, device_id_type=MESH)
    lax.fori_loop(1, CP, greet, 0)

    def product(n, c):
        return jnp.dot(
            heads_ref[...], wo[n, :, c * CW : (c + 1) * CW], preferred_element_type=jnp.float32
        )

    def remote(n, src, dst, target):
        return pltpu.make_async_remote_copy(
            src_ref=src,
            dst_ref=dst,
            send_sem=z_send.at[n],
            recv_sem=z_recv.at[n],
            device_id={"tp": target},
            device_id_type=MESH,
        )

    half = ROWS // 2
    far_copies, near_copies = [], []
    for c in range(CHUNKS):
        far_copies.append(
            (
                remote(4 * c, far.at[c, pl.ds(0, half)], far_in.at[c, 0], up),
                remote(4 * c + 1, far.at[c, pl.ds(half, half)], far_in.at[c, 1], down),
            )
        )
        near_copies.append(
            (
                remote(4 * c + 2, near.at[c, 0], near_in.at[c, 0], up),
                remote(4 * c + 3, near.at[c, 1], near_in.at[c, 1], down),
            )
        )

    def send_far(c):
        far[c] = product(0, c).astype(jnp.bfloat16)
        for copy in far_copies[c]:
            copy.start()

    def send_near(c):
        to_up, to_down = product(1, c), product(2, c)
        far_copies[c][0].wait_recv()
        near[c, 0, :half] = (to_up[:half] + far_in[c, 0].astype(jnp.float32)).astype(jnp.bfloat16)
        near[c, 0, half:] = to_up[half:].astype(jnp.bfloat16)
        near_copies[c][0].start()
        far_copies[c][1].wait_recv()
        near[c, 1, :half] = to_down[:half].astype(jnp.bfloat16)
        near[c, 1, half:] = (to_down[half:] + far_in[c, 1].astype(jnp.float32)).astype(
            jnp.bfloat16
        )
        near_copies[c][1].start()

    row = lax.broadcasted_iota(jnp.int32, (ROWS, ROWS), 0)
    column = lax.broadcasted_iota(jnp.int32, (ROWS, ROWS), 1)
    to_owner = (row == slot_ref[...]).astype(jnp.float32).astype(jnp.bfloat16)
    origin = (lax.rem(row, BLOCK) // 4) * 8 + (row // BLOCK) * 4 + lax.rem(row, 4)
    to_place = (column == origin).astype(jnp.float32).astype(jnp.bfloat16)

    def acopy(c, k, target, slot):
        return pltpu.make_async_remote_copy(
            src_ref=spread.at[c, target],
            dst_ref=landed.at[c, slot],
            send_sem=a_send.at[c, k],
            recv_sem=a_recv.at[c, k],
            device_id={"cp": target},
            device_id_type=MESH,
        )

    def finish_sum(c):
        for copy in near_copies[c]:
            copy.wait_recv()
        total = (
            own_sum[c]
            + near_in[c, 0].astype(jnp.float32)
            + near_in[c, 1].astype(jnp.float32)
        ).astype(jnp.bfloat16)
        picked = jnp.dot(to_owner, total, preferred_element_type=jnp.float32)
        spread[c] = picked.reshape(CP, 8, CW).astype(jnp.bfloat16)
        landed[c, me] = spread[c, me]

        def send(k, carry):
            acopy(c, k, lax.rem(me + k, CP), me).start()
            return carry

        lax.fori_loop(1, CP, send, 0)

    def place(c):
        def wait(k, carry):
            copy = acopy(c, k, lax.rem(me + k, CP), lax.rem(me + CP - k, CP))
            copy.wait_send()
            copy.wait_recv()
            return carry

        lax.fori_loop(1, CP, wait, 0)
        rows = landed[c].astype(jnp.float32).reshape(ROWS, CW).astype(jnp.bfloat16)
        out_ref[:, c * CW : (c + 1) * CW] = jnp.dot(
            to_place, rows, preferred_element_type=jnp.float32
        ).astype(jnp.bfloat16)

    loads[0].wait()
    far[0] = product(0, 0).astype(jnp.bfloat16)
    pl.semaphore_wait(barrier, CP + 1)
    for copy in far_copies[0]:
        copy.start()
    send_far(1)
    loads[1].wait()
    loads[2].wait()
    send_near(0)
    send_far(2)
    send_near(1)
    send_far(3)
    loads[3].wait()
    own_sum[0] = product(3, 0)
    send_near(2)
    own_sum[1] = product(3, 1)
    send_near(3)
    own_sum[2] = product(3, 2)
    own_sum[3] = product(3, 3)
    for c in range(CHUNKS):
        finish_sum(c)
        if c > 0:
            place(c - 1)
    place(CHUNKS - 1)
    for c in range(CHUNKS):
        for copy in (*far_copies[c], *near_copies[c]):
            copy.wait_send()


def output_call(slot_rows, heads, wo):
    vmem = pl.BlockSpec(memory_space=pltpu.VMEM)
    dma = pltpu.SemaphoreType.DMA
    half = ROWS // 2
    bf16 = jnp.bfloat16
    return pl.pallas_call(
        output_kernel,
        out_shape=jax.ShapeDtypeStruct((ROWS, WIDTH), bf16),
        in_specs=[vmem, vmem, pl.BlockSpec(memory_space=pl.ANY)],
        out_specs=vmem,
        scratch_shapes=[
            pltpu.VMEM((TP, WIDTH, WIDTH), bf16),
            pltpu.VMEM((CHUNKS, ROWS, CW), bf16),
            pltpu.VMEM((CHUNKS, 2, ROWS, CW), bf16),
            pltpu.VMEM((CHUNKS, 2, half, CW), bf16),
            pltpu.VMEM((CHUNKS, 2, ROWS, CW), bf16),
            pltpu.VMEM((CHUNKS, CP, 8, CW), bf16),
            pltpu.VMEM((CHUNKS, CP, 8, CW), bf16),
            pltpu.VMEM((CHUNKS, ROWS, CW), jnp.float32),
            dma((4,)), dma((4 * CHUNKS,)), dma((4 * CHUNKS,)), dma((CHUNKS, CP)), dma((CHUNKS, CP)),
        ],
        compiler_params=pltpu.CompilerParams(
            collective_id=1, has_side_effects=True, vmem_limit_bytes=40 * 1024 * 1024
        ),
        name="project_out",
    )(slot_rows, heads, wo)


def local(hidden, query_weight, key_matrix, value_matrix, output_weight, bounds, block_owner):
    inverse = rope_inverse(HEAD)
    inverse = jnp.concatenate([inverse, inverse])[None, :]
    slots = slots_of(block_owner)
    slot_rows = (slots[:, None] * PORTION + jnp.arange(PORTION, dtype=jnp.int32)[None, :]).reshape(
        1, ROWS
    )
    keys, values, queries = gather_call(
        bounds, hidden, query_weight, key_matrix, value_matrix, inverse
    )
    heads = attend_call(
        bounds,
        queries.reshape(ROWS, WIDTH),
        keys.reshape(TOKENS, HEAD),
        values.reshape(TOKENS, HEAD),
    )
    return output_call(slot_rows, heads, output_weight)


def solution(mesh):
    placed = (P("cp", "tp"), P(None, "tp"), P(None, "tp"), P(None, "tp"), P("tp", None), P(), P())
    return jax.shard_map(
        local, mesh=mesh, in_specs=placed, out_specs=P("cp", "tp"), check_vma=False
    )
```

profile of v0, /device:TPU:1, one launch (start us, length us, event | category | flops | bytes accessed | tf_op | source)
XLA Modules:
  0.0 133.6 jit_solution(965896290973144965)
XLA Ops:
  0.0 0.0 copy-start.7
  0.0 0.1 maximum_bitcast_fusion.inverse_ref
  0.1 0.0 copy-start.3
  0.1 1.2 copy-done.3
  1.3 0.0 copy-start.4
  1.3 1.2 copy-done.4
  2.6 0.0 copy-start.5
  2.6 1.0 copy-done.5
  3.6 0.0 copy-start.6
  3.6 0.7 copy-done.6
  4.3 59.2 %gather_project.1 = (bf16[4,4,2,2,128,128]{5,4,3,2,1,0:T(8,128)(2,1)}, bf16[4,4,2,2,128,128]{5,4,3,2,1,0:T(8,128)(2,1)}, bf16[32,8,1024]{2,1,0:T(8,128)(2,1)S(1)}) custom-call(s32[9]{0:T(128)S(1)} %copy-done.6, bf16[256,1024]{1,0:T(8,128)(2,1)S(1)} %copy-done.5, bf16[4096,1024]{1,0:T(8,128)(2,1)} %wq_ref.1, bf16[4096,128]{1,0:T(8,128)(2,1)S(1)} %copy-done.3, ...), custom_call_target="tpu_custom_call" | custom-call | tf_op jit(solution)/shard_map/gather_project/pallas_call | solution.py:332
  63.4 0.0 copy-start.1
  63.4 1.6 %copy-done.1 = bf16[4,4,2,2,128,128]{5,4,3,2,1,0:T(8,128)(2,1)S(1)} copy-done((bf16[4,4,2,2,128,128]{5,4,3,2,1,0:T(8,128)(2,1)S(1)}, bf16[4,4,2,2,128,128]{5,4,3,2,1,0:T(8,128)(2,1)}, u32[]{:S(2)}) %copy-start.1) | copy-done | bytes 2097176
  65.0 0.0 copy-start.2
  65.0 1.6 %copy-done.2 = bf16[4,4,2,2,128,128]{5,4,3,2,1,0:T(8,128)(2,1)S(1)} copy-done((bf16[4,4,2,2,128,128]{5,4,3,2,1,0:T(8,128)(2,1)S(1)}, bf16[4,4,2,2,128,128]{5,4,3,2,1,0:T(8,128)(2,1)}, u32[]{:S(2)}) %copy-start.2) | copy-done | bytes 2097176
  66.6 27.3 %attend.1.heads_ref = bf16[256,1024]{1,0:T(8,128)(2,1)S(1)} custom-call(s32[9]{0:T(128)S(1)} %copy-done.6, bf16[256,1024]{1,0:T(8,128)(2,1)S(1)} %bitcast.7, bf16[8192,128]{1,0:T(8,128)(2,1)S(1)} %bitcast.5, bf16[8192,128]{1,0:T(8,128)(2,1)S(1)} %bitcast.6), custom_call_target="tpu_custom_call" | custom-call | tf_op jit(solution)/shard_map/attend/pallas_call | solution.py:419
  93.9 0.0 copy-done.7
  93.9 0.2 convert_reduce_fusion
  94.1 0.1 iota_add_fusion
  94.2 0.1 add.36.slot_ref
  94.3 0.0 copy-start
  94.3 3.4 %copy-done = bf16[1024,4096]{1,0:T(8,128)(2,1)S(1)} copy-done((bf16[1024,4096]{1,0:T(8,128)(2,1)S(1)}, bf16[1024,4096]{1,0:T(8,128)(2,1)}, u32[]{:S(2)}) %copy-start) | copy-done | bytes 8388632
  97.7 35.1 %project_out.1 = bf16[256,1024]{1,0:T(8,128)(2,1)S(1)} custom-call(s32[1,256]{1,0:T(1,128)S(1)} %add.36.slot_ref, bf16[256,1024]{1,0:T(8,128)(2,1)S(1)} %attend.1.heads_ref, bf16[1024,4096]{1,0:T(8,128)(2,1)S(1)} %copy-done), custom_call_target="tpu_custom_call" | custom-call | tf_op jit(solution)/shard_map/project_out/pallas_call | solution.py:590
  132.8 0.8 copy.9
  (2 shorter events, 0.0 us)
Async XLA Ops:
  0.0 93.9 %copy-start.7 = (s32[64]{0:T(128)S(1)}, s32[64]{0:T(128)}, u32[]{:S(2)}) copy-start(s32[64]{0:T(128)} %param.13) | copy-start | bytes 772
  0.1 1.2 copy-start.3
  1.3 1.2 copy-start.4
  2.6 1.0 copy-start.5
  3.6 0.7 copy-start.6
  63.4 1.6 %copy-start.1 = (bf16[4,4,2,2,128,128]{5,4,3,2,1,0:T(8,128)(2,1)S(1)}, bf16[4,4,2,2,128,128]{5,4,3,2,1,0:T(8,128)(2,1)}, u32[]{:S(2)}) copy-start(bf16[4,4,2,2,128,128]{5,4,3,2,1,0:T(8,128)(2,1)} %get-tuple-element.9) | copy-start | bytes 6291460
  65.0 1.6 %copy-start.2 = (bf16[4,4,2,2,128,128]{5,4,3,2,1,0:T(8,128)(2,1)S(1)}, bf16[4,4,2,2,128,128]{5,4,3,2,1,0:T(8,128)(2,1)}, u32[]{:S(2)}) copy-start(bf16[4,4,2,2,128,128]{5,4,3,2,1,0:T(8,128)(2,1)} %get-tuple-element.10) | copy-start | bytes 6291460
  94.3 3.4 %copy-start = (bf16[1024,4096]{1,0:T(8,128)(2,1)S(1)}, bf16[1024,4096]{1,0:T(8,128)(2,1)}, u32[]{:S(2)}) copy-start(bf16[1024,4096]{1,0:T(8,128)(2,1)} %wo_ref.1) | copy-start | bytes 25165828
where the time goes:
time: 131 us; the launch traced here: 134 us
  Pallas kernels  122 us (93%)
  local copies, waits for them, and re-layouts  11.6 us (9%)
    pallas_call x1, Pallas kernels, gather_call(): pl.pallas_call(gather_kernel, out_shape=(kv, kv, jax.ShapeDtypeStruct((CP...  59.2 us
    pallas_call x1, Pallas kernels, output_call(): pl.pallas_call(output_kernel, out_shape=jax.ShapeDtypeStruct((ROWS, WIDTH...  35.1 us
    pallas_call x1, Pallas kernels, attend_call(): pl.pallas_call(attend_kernel, out_shape=jax.ShapeDtypeStruct((ROWS, WIDTH...  27.3 us
    unnamed x17, local copies, waits for them, and re-layouts  11.5 us

commit v1 on v0

--- a/solution.py
+++ b/solution.py
@@ -52,9 +52,15 @@
     return start
 
 
+PARTS = 4
+PART = ROWS // PARTS
+SPAN = 8
+PENALTY = -1e30
+
+
 def gather_kernel(
     bounds_ref, hidden_ref, wq_ref, wk_ref, wv_ref, inverse_ref,
-    k_ref, v_ref, q_ref,
+    k_ref, v_ref, q_ref, mark_ref,
     full, wq, wkv, qtmp, qsend, cosine, sine,
     w_sem, z_send, z_recv, g_send, g_recv, q_send, q_recv,
 ):
@@ -65,12 +71,15 @@
     xcoord = me // 8
     partner = me + 1 - 2 * core
     up, down = lax.rem(tp + 1, TP), lax.rem(tp + 3, TP)
-
+    own_columns = pl.ds(pl.multiple_of(tp * WIDTH, WIDTH), WIDTH)
+
+    bring = pltpu.make_async_copy(hidden_ref, full.at[:, own_columns], w_sem.at[3])
     weights = [
         pltpu.make_async_copy(wk_ref, wkv.at[:, pl.ds(0, HEAD)], w_sem.at[0]),
         pltpu.make_async_copy(wv_ref, wkv.at[:, pl.ds(HEAD, HEAD)], w_sem.at[1]),
         pltpu.make_async_copy(wq_ref, wq, w_sem.at[2]),
     ]
+    bring.start()
     for copy in weights:
         copy.start()
 
@@ -85,92 +94,97 @@
     pl.semaphore_signal(barrier, inc=1, device_id={"tp": up}, device_id_type=MESH)
     pl.semaphore_signal(barrier, inc=1, device_id={"tp": down}, device_id_type=MESH)
     lax.fori_loop(1, CP, greet, 0)
+    bring.wait()
     pl.semaphore_wait(barrier, CP + 1)
 
-    def zcopy(n, source, target, owner, row, count):
+    def zcopy(n, target, owner, row, count):
         columns = pl.ds(pl.multiple_of(owner * WIDTH, WIDTH), WIDTH)
-        source_ref = (
-            hidden_ref.at[pl.ds(row, count), :]
-            if source
-            else full.at[pl.ds(row, count), columns]
-        )
+        ref = full.at[pl.ds(row, count), columns]
         return pltpu.make_async_remote_copy(
-            src_ref=source_ref,
-            dst_ref=full.at[pl.ds(row, count), columns],
+            src_ref=ref,
+            dst_ref=ref,
             send_sem=z_send.at[n],
             recv_sem=z_recv.at[n],
             device_id={"tp": target},
             device_id_type=MESH,
         )
 
-    own = {}
-    for n, (row, count) in enumerate(((0, 128), (128, 64), (192, 64))):
-        own[n] = (
-            zcopy(2 * n, True, up, tp, row, count),
-            zcopy(2 * n + 1, True, down, tp, row, count),
-        )
-    fwd = {
-        r: (
-            zcopy(6 + 2 * r, False, up, down, r * 128, 64),
-            zcopy(7 + 2 * r, False, down, up, r * 128 + 64, 64),
-        )
-        for r in range(2)
-    }
-    for n in (0, 1):
-        for copy in own[n]:
+    half = PART // 2
+    own = [
+        (
+            zcopy(4 * r, up, tp, r * PART, PART),
+            zcopy(4 * r + 1, down, tp, r * PART, PART),
+        )
+        for r in range(PARTS)
+    ]
+    fwd = [
+        (
+            zcopy(4 * r + 2, down, up, r * PART, half),
+            zcopy(4 * r + 3, up, down, r * PART + half, half),
+        )
+        for r in range(PARTS)
+    ]
+    for copy in (*own[0], *own[1]):
+        copy.start()
+
+    def relay_z(r):
+        for copy in own[r]:
+            copy.wait_recv()
+        for copy in fwd[r]:
             copy.start()
-
-    full[:, pl.ds(pl.multiple_of(tp * WIDTH, WIDTH), WIDTH)] = hidden_ref[...]
+        if r + 2 < PARTS:
+            for copy in own[r + 2]:
+                copy.start()
+
+    lanes = lax.broadcasted_iota(jnp.int32, (BLOCK, HEAD), 1)
+    sublanes = lax.broadcasted_iota(jnp.int32, (BLOCK, HEAD), 0)
     inverse = inverse_ref[...]
-    lanes = lax.broadcasted_iota(jnp.int32, (BLOCK, HEAD), 1)
     for r in range(2):
-        tokens = me * ROWS + r * BLOCK + lax.broadcasted_iota(jnp.int32, (BLOCK, HEAD), 0)
+        tokens = me * ROWS + r * BLOCK + sublanes
         angle = (tokens - starts_of(tokens, bounds_ref)).astype(jnp.float32) * inverse
         turn = jnp.sin(angle)
         cosine[pl.ds(r * BLOCK, BLOCK), :] = jnp.cos(angle)
         sine[pl.ds(r * BLOCK, BLOCK), :] = jnp.where(lanes < HEAD // 2, -turn, turn)
+
+    place = jnp.minimum(jnp.maximum(sublanes - me * PORTION, 0), PORTION)
+
+    def mark(b, carry):
+        tokens = b * BLOCK + sublanes
+        document = jnp.zeros_like(tokens)
+        for i in range(1, 8):
+            document = jnp.where(tokens >= bounds_ref[i], i, document)
+        spot = 8 + lax.rem(b, SPAN) * (PORTION + 1) + place
+        hit = (lanes == document) | (lanes == spot)
+        mark_ref[pl.ds(pl.multiple_of(b * BLOCK, BLOCK), BLOCK), :] = (
+            hit.astype(jnp.float32).astype(jnp.bfloat16)
+        )
+        return carry
+
+    lax.fori_loop(0, NBLK // 2, mark, 0)
     weights[0].wait()
     weights[1].wait()
-
-    for copy in own[0]:
-        copy.wait_recv()
-    for copy in fwd[0]:
-        copy.start()
-    for copy in own[2]:
-        copy.start()
     weights[2].wait()
 
-    def rotate(raw, r):
-        table = pl.ds(r * BLOCK, BLOCK)
+    def rotate(raw, row, count):
+        table = pl.ds(row, count)
         return raw * cosine[table, :] + pltpu.roll(raw, HEAD // 2, 1) * sine[table, :]
 
-    def keys_values(r):
-        raw = jnp.dot(
-            full[pl.ds(r * BLOCK, BLOCK), :], wkv[...], preferred_element_type=jnp.float32
-        )
-        k_ref[xcoord, ycoord, core, r] = rotate(raw[:, :HEAD], r).astype(jnp.bfloat16)
-        v_ref[xcoord, ycoord, core, r] = raw[:, HEAD:].astype(jnp.bfloat16)
-
-    def queries(r):
-        def pair(n, carry):
-            columns = pl.ds(pl.multiple_of(n * 2 * HEAD, 2 * HEAD), 2 * HEAD)
-            raw = jnp.dot(
-                full[pl.ds(r * BLOCK, BLOCK), :],
-                wq[:, columns],
-                preferred_element_type=jnp.float32,
-            )
-            turned = jnp.concatenate(
-                [rotate(raw[:, :HEAD], r), rotate(raw[:, HEAD:], r)], axis=1
-            )
-            qtmp[pl.ds(r * BLOCK, BLOCK), columns] = turned.astype(jnp.bfloat16)
-            return carry
-
-        lax.fori_loop(0, WIDTH // (2 * HEAD), pair, 0)
+    def queries(r, n):
+        columns = slice(n * 2 * HEAD, (n + 1) * 2 * HEAD)
+        rows = pl.ds(r * BLOCK, BLOCK)
+        raw = jnp.dot(full[rows, :], wq[:, columns], preferred_element_type=jnp.float32)
+        turned = jnp.concatenate(
+            [rotate(raw[:, :HEAD], r * BLOCK, BLOCK), rotate(raw[:, HEAD:], r * BLOCK, BLOCK)],
+            axis=1,
+        )
+        qtmp[pl.ds((n // 2) * BLOCK, BLOCK), (n % 2) * 2 * HEAD : (n % 2 + 1) * 2 * HEAD] = (
+            turned.astype(jnp.bfloat16)
+        )
 
     def gather(which, r):
         buffer = (k_ref, v_ref)[which]
         a, b = ((xcoord, ycoord), (ycoord, xcoord))[which]
-        base = (which * 2 + r) * 12
+        base = (which * PARTS + r) * 12
 
         def neighbour(along, step):
             if along == 0:
@@ -207,12 +221,12 @@
         b_far = lax.rem(b + 2, 4)
         return dict(
             ring1=(
-                copy(0, piece(a, 0, BLOCK), neighbour(0, 1)),
-                copy(1, piece(a, 0, BLOCK), neighbour(0, 3)),
+                copy(0, piece(a, 0, PART), neighbour(0, 1)),
+                copy(1, piece(a, 0, PART), neighbour(0, 3)),
             ),
             ring1_far=(
-                copy(2, piece(a_prev, 0, 64), neighbour(0, 1)),
-                copy(3, piece(a_next, 64, 64), neighbour(0, 3)),
+                copy(2, piece(a_prev, 0, half), neighbour(0, 1)),
+                copy(3, piece(a_next, half, half), neighbour(0, 3)),
             ),
             ring2=(
                 copy(4, line(b, 0, 4), neighbour(1, 1)),
@@ -230,7 +244,7 @@
             ),
         )
 
-    flows = {r: [gather(which, r) for which in range(2)] for r in range(2)}
+    flows = [[gather(which, r) for which in range(2)] for r in range(PARTS)]
 
     def start(r, name):
         for flow in flows[r]:
@@ -247,183 +261,231 @@
             for n in which:
                 flow["across"][n].start()
 
-    for copy in fwd[0]:
-        copy.wait_recv()
-    keys_values(0)
-    start(0, "ring1")
-    for n in (1, 2):
-        for copy in own[n]:
+    def s0(r):
+        for copy in fwd[r]:
             copy.wait_recv()
-    for copy in fwd[1]:
-        copy.start()
-    queries(0)
-    arrived(0, "ring1")
-    start(0, "ring1_far")
-    arrived(0, "ring1_far")
-    start(0, "ring2")
-    across(0, (0,))
-    for copy in fwd[1]:
-        copy.wait_recv()
-    keys_values(1)
-    start(1, "ring1")
-    arrived(0, "ring2")
-    start(0, "ring2_far")
-    across(0, (1, 2))
-    queries(1)
-    arrived(1, "ring1")
-    start(1, "ring1_far")
+        raw = jnp.dot(
+            full[pl.ds(r * PART, PART), :], wkv[...], preferred_element_type=jnp.float32
+        )
+        k_ref[xcoord, ycoord, core, r] = rotate(raw[:, :HEAD], r * PART, PART).astype(
+            jnp.bfloat16
+        )
+        v_ref[xcoord, ycoord, core, r] = raw[:, HEAD:].astype(jnp.bfloat16)
+        start(r, "ring1")
+
+    def s1(r):
+        arrived(r, "ring1")
+        start(r, "ring1_far")
+
+    def s2(r):
+        arrived(r, "ring1_far")
+        start(r, "ring2")
+        across(r, (0,))
+
+    def s3(r):
+        arrived(r, "ring2")
+        start(r, "ring2_far")
+        across(r, (1, 2))
+
+    def s4(r):
+        arrived(r, "ring2_far")
+        across(r, (3,))
 
     out_row = lax.broadcasted_iota(jnp.int32, (ROWS, ROWS), 0)
     in_row = lax.broadcasted_iota(jnp.int32, (ROWS, ROWS), 1)
     origin = lax.rem(out_row // 4, 2) * BLOCK + (out_row // 8) * 4 + lax.rem(out_row, 4)
     pick = (in_row == origin).astype(jnp.float32).astype(jnp.bfloat16)
-    ordered = jnp.dot(pick, qtmp[...], preferred_element_type=jnp.float32)
-    qsend[...] = ordered.reshape(CP, 8, WIDTH).astype(jnp.bfloat16)
-    q_ref[me] = qsend[me]
-
-    def qcopy(k, target, slot):
+
+    def qcopy(r, k, target, slot):
         return pltpu.make_async_remote_copy(
-            src_ref=qsend.at[target],
-            dst_ref=q_ref.at[slot],
-            send_sem=q_send.at[k],
-            recv_sem=q_recv.at[k],
+            src_ref=qsend.at[r, target],
+            dst_ref=q_ref.at[slot, r],
+            send_sem=q_send.at[r, k],
+            recv_sem=q_recv.at[r, k],
             device_id={"cp": target},
             device_id_type=MESH,
         )
 
-    def send_queries(k, carry):
-        qcopy(k, lax.rem(me + k, CP), me).start()
-        return carry
-
-    def wait_queries(k, carry):
-        copy = qcopy(k, lax.rem(me + k, CP), lax.rem(me + CP - k, CP))
-        copy.wait_send()
-        copy.wait_recv()
-        return carry
-
-    arrived(1, "ring1_far")
-    start(1, "ring2")
-    across(1, (0,))
-    lax.fori_loop(1, CP, send_queries, 0)
-    arrived(0, "ring2_far")
-    across(0, (3,))
-    arrived(1, "ring2")
-    start(1, "ring2_far")
-    across(1, (1, 2))
-    arrived(1, "ring2_far")
-    across(1, (3,))
-    lax.fori_loop(1, CP, wait_queries, 0)
-    for r in range(2):
+    def spread(r):
+        ordered = jnp.dot(pick, qtmp[...], preferred_element_type=jnp.float32)
+        qsend[r] = ordered.reshape(CP, 8, WIDTH // 2).astype(jnp.bfloat16)
+        q_ref[me, r] = qsend[r, me]
+
+        def send(k, carry):
+            qcopy(r, k, lax.rem(me + k, CP), me).start()
+            return carry
+
+        lax.fori_loop(1, CP, send, 0)
+
+    def spread_done(r):
+        def wait(k, carry):
+            copy = qcopy(r, k, lax.rem(me + k, CP), lax.rem(me + CP - k, CP))
+            copy.wait_send()
+            copy.wait_recv()
+            return carry
+
+        lax.fori_loop(1, CP, wait, 0)
+
+    relay_z(0)
+    lax.fori_loop(NBLK // 2, NBLK, mark, 0)
+    relay_z(1)
+    s0(0)
+    s1(0)
+    relay_z(2)
+    s2(0)
+    s0(1)
+    queries(0, 0)
+    queries(0, 1)
+    s1(1)
+    relay_z(3)
+    s3(0)
+    queries(0, 2)
+    s2(1)
+    s0(2)
+    queries(0, 3)
+    spread(0)
+    s4(0)
+    s0(3)
+    s1(2)
+    s3(1)
+    queries(1, 0)
+    s1(3)
+    s2(2)
+    queries(1, 1)
+    s4(1)
+    queries(1, 2)
+    s2(3)
+    queries(1, 3)
+    spread(1)
+    s3(2)
+    s3(3)
+    s4(2)
+    s4(3)
+    spread_done(0)
+    spread_done(1)
+    for r in range(PARTS):
         arrived(r, "across")
         for flow in flows[r]:
             for name in ("ring1", "ring1_far", "ring2", "ring2_far", "across"):
                 for copy in flow[name]:
                     copy.wait_send()
-    for group in (*own.values(), *fwd.values()):
+    for group in (*own, *fwd):
         for copy in group:
             copy.wait_send()
 
 
 def gather_call(bounds, hidden, wq, wk, wv, inverse):
     vmem = pl.BlockSpec(memory_space=pltpu.VMEM)
-    anywhere = pl.BlockSpec(memory_space=pl.ANY)
-    kv = jax.ShapeDtypeStruct((4, 4, 2, 2, BLOCK, HEAD), jnp.bfloat16)
+    hbm = pl.BlockSpec(memory_space=pltpu.HBM)
+    kv = jax.ShapeDtypeStruct((4, 4, 2, PARTS, PART, HEAD), jnp.bfloat16)
     dma = pltpu.SemaphoreType.DMA
     return pl.pallas_call(
         gather_kernel,
-        out_shape=(kv, kv, jax.ShapeDtypeStruct((CP, 8, WIDTH), jnp.bfloat16)),
-        in_specs=[
-            pl.BlockSpec(memory_space=pltpu.SMEM), vmem, anywhere, anywhere, anywhere, vmem,
-        ],
-        out_specs=(vmem, vmem, vmem),
+        out_shape=(
+            kv,
+            kv,
+            jax.ShapeDtypeStruct((CP, 2, 8, WIDTH // 2), jnp.bfloat16),
+            jax.ShapeDtypeStruct((TOKENS, HEAD), jnp.bfloat16),
+        ),
+        in_specs=[pl.BlockSpec(memory_space=pltpu.SMEM), hbm, hbm, hbm, hbm, vmem],
+        out_specs=(vmem, vmem, vmem, vmem),
         scratch_shapes=[
             pltpu.VMEM((ROWS, TP * WIDTH), jnp.bfloat16),
             pltpu.VMEM((TP * WIDTH, WIDTH), jnp.bfloat16),
             pltpu.VMEM((TP * WIDTH, 2 * HEAD), jnp.bfloat16),
-            pltpu.VMEM((ROWS, WIDTH), jnp.bfloat16),
-            pltpu.VMEM((CP, 8, WIDTH), jnp.bfloat16),
+            pltpu.VMEM((ROWS, WIDTH // 2), jnp.bfloat16),
+            pltpu.VMEM((2, CP, 8, WIDTH // 2), jnp.bfloat16),
             pltpu.VMEM((ROWS, HEAD), jnp.float32),
             pltpu.VMEM((ROWS, HEAD), jnp.float32),
-            dma((3,)), dma((10,)), dma((10,)), dma((48,)), dma((48,)), dma((CP,)), dma((CP,)),
+            dma((4,)), dma((4 * PARTS,)), dma((4 * PARTS,)),
+            dma((24 * PARTS,)), dma((24 * PARTS,)), dma((2, CP)), dma((2, CP)),
         ],
         compiler_params=pltpu.CompilerParams(
-            collective_id=0, has_side_effects=True, vmem_limit_bytes=50 * 1024 * 1024
+            collective_id=0, has_side_effects=True, vmem_limit_bytes=32 * 1024 * 1024
         ),
         name="gather_project",
     )(bounds, hidden, wq, wk, wv, inverse)
 
 
-GROUP = 8
-TILE = 512
-
-
-def attend_kernel(bounds_ref, q_ref, k_ref, v_ref, o_ref):
+TILE = SPAN * BLOCK
+
+
+def attend_kernel(bounds_ref, q_ref, k_ref, v_ref, mark_ref, o_ref):
+    rows = SPAN * 8
+    count = 4 * rows
+    factor = math.log2(math.e) / math.sqrt(HEAD)
+    row = lax.rem(lax.broadcasted_iota(jnp.int32, (count, HEAD), 0), rows)
+    lane = lax.broadcasted_iota(jnp.int32, (count, HEAD), 1)
+    block, step = row // 8, lax.rem(row, PORTION)
+    key_block, key_step = (lane - 8) // (PORTION + 1), lax.rem(lane - 8, PORTION + 1)
+    later = (key_block > block) | ((key_block == block) & (key_step > step))
+    later = later & (lane >= 8) & (lane < 8 + SPAN * (PORTION + 1))
     me = lax.axis_index("cp")
-    rows = GROUP * PORTION
-    scale = 1.0 / math.sqrt(HEAD)
+    ones = jnp.ones((TILE, HEAD), jnp.bfloat16)
 
     def group(g, carry):
         first = pl.multiple_of(g * rows, rows)
-        q = jnp.concatenate(
-            [q_ref[pl.ds(first, rows), h * HEAD : (h + 1) * HEAD] for h in range(HEADS)], axis=0
-        )
-        row = lax.rem(lax.broadcasted_iota(jnp.int32, (HEADS * rows, 1), 0), rows)
-        tokens = (g * GROUP + row // PORTION) * BLOCK + me * PORTION + lax.rem(row, PORTION)
-        starts = starts_of(tokens, bounds_ref)
-        low_token = g * GROUP * BLOCK
+        tokens = (g * SPAN + block) * BLOCK + me * PORTION + step
+        document = jnp.zeros_like(tokens)
         low = jnp.int32(0)
         for i in range(1, 8):
-            low = jnp.where(low_token >= bounds_ref[i], bounds_ref[i], low)
-
-        def tile(j, state):
-            top, total, mixed = state
+            document = jnp.where(tokens >= bounds_ref[i], i, document)
+            low = jnp.where(g * TILE >= bounds_ref[i], bounds_ref[i], low)
+        other = (lane < 8) & (lane != document)
+        q = jnp.concatenate(
+            [q_ref[pl.ds(first, rows), h * HEAD : (h + 1) * HEAD] for h in range(4)], axis=0
+        )
+        inner = jnp.where(other, PENALTY, 0.0).astype(jnp.bfloat16)
+        outer = jnp.where(other | later, PENALTY, 0.0).astype(jnp.bfloat16)
+
+        def scores_of(j, penalties):
             at = pl.ds(pl.multiple_of(j * TILE, TILE), TILE)
-            scores = lax.dot_general(
-                q, k_ref[at, :], (((1,), (1,)), ((), ())), preferred_element_type=jnp.float32
+            return lax.dot_general(
+                jnp.concatenate([q, penalties], axis=1),
+                jnp.concatenate([k_ref[at, :], mark_ref[at, :]], axis=1),
+                (((1,), (1,)), ((), ())),
+                preferred_element_type=jnp.float32,
+            ) * factor
+
+        def mix(j, scores, top):
+            at = pl.ds(pl.multiple_of(j * TILE, TILE), TILE)
+            weights = jnp.exp2(scores - top).astype(jnp.bfloat16)
+            return jnp.dot(
+                weights,
+                jnp.concatenate([v_ref[at, :], ones], axis=1),
+                preferred_element_type=jnp.float32,
             )
-            keys = j * TILE + lax.broadcasted_iota(jnp.int32, (HEADS * rows, TILE), 1)
-            allowed = (keys >= starts) & (keys <= tokens)
-            scores = jnp.where(allowed, scores * scale, masked_score)
+
+        scores = scores_of(g, outer)
+        top = jnp.max(scores, axis=1, keepdims=True)
+        mixed = mix(g, scores, top)
+
+        def tile(n, state):
+            top, mixed = state
+            j = g - 1 - n
+            scores = scores_of(j, inner)
             new_top = jnp.maximum(top, jnp.max(scores, axis=1, keepdims=True))
-            weights = jnp.where(allowed, jnp.exp(scores - new_top), 0.0)
-            factor = jnp.exp(top - new_top)
-            part = weights[:, :HEAD]
-            for c in range(1, TILE // HEAD):
-                part = part + weights[:, c * HEAD : (c + 1) * HEAD]
-            total = total * factor + part
-            mixed = mixed * factor + jnp.dot(
-                weights.astype(jnp.bfloat16), v_ref[at, :], preferred_element_type=jnp.float32
-            )
-            return new_top, total, mixed
-
-        top, total, mixed = lax.fori_loop(
-            low // TILE,
-            (g + 1) * (GROUP * BLOCK // TILE),
-            tile,
-            (
-                jnp.full((HEADS * rows, 1), masked_score, jnp.float32),
-                jnp.zeros((HEADS * rows, HEAD), jnp.float32),
-                jnp.zeros((HEADS * rows, HEAD), jnp.float32),
-            ),
-        )
-        out = (mixed / jnp.sum(total, axis=1, keepdims=True)).astype(jnp.bfloat16)
-        for h in range(HEADS):
+            return new_top, mixed * jnp.exp2(top - new_top) + mix(j, scores, new_top)
+
+        top, mixed = lax.fori_loop(0, g - low // TILE, tile, (top, mixed))
+        out = (mixed[:, :HEAD] / mixed[:, HEAD:]).astype(jnp.bfloat16)
+        for h in range(4):
             o_ref[pl.ds(first, rows), h * HEAD : (h + 1) * HEAD] = out[h * rows : (h + 1) * rows]
         return carry
 
-    lax.fori_loop(0, NBLK // GROUP, group, 0)
-
-
-def attend_call(bounds, q, k, v):
+    lax.fori_loop(0, NBLK // SPAN, group, 0)
+
+
+def attend_call(bounds, q, k, v, marks):
     vmem = pl.BlockSpec(memory_space=pltpu.VMEM)
     return pl.pallas_call(
         attend_kernel,
-        out_shape=jax.ShapeDtypeStruct((ROWS, WIDTH), jnp.bfloat16),
-        in_specs=[pl.BlockSpec(memory_space=pltpu.SMEM), vmem, vmem, vmem],
+        out_shape=jax.ShapeDtypeStruct((2 * ROWS, WIDTH // 2), jnp.bfloat16),
+        in_specs=[pl.BlockSpec(memory_space=pltpu.SMEM), vmem, vmem, vmem, vmem],
         out_specs=vmem,
-        compiler_params=pltpu.CompilerParams(vmem_limit_bytes=40 * 1024 * 1024),
+        compiler_params=pltpu.CompilerParams(vmem_limit_bytes=20 * 1024 * 1024),
         name="attend",
-    )(bounds, q, k, v)
+    )(bounds, q, k, v, marks)
 
 
 CHUNKS = 4
@@ -432,7 +494,7 @@
 
 def output_kernel(
     slot_ref, heads_ref, wo_ref, out_ref,
-    wo, far, near, far_in, near_in, spread, landed, own_sum,
+    heads, wo, far, near, far_in, near_in, spread, landed, own_sum,
     w_sem, z_send, z_recv, a_send, a_recv,
 ):
     me = lax.axis_index("cp")
@@ -457,9 +519,18 @@
     pl.semaphore_signal(barrier, inc=1, device_id={"tp": down}, device_id_type=MESH)
     lax.fori_loop(1, CP, greet, 0)
 
+    wide_row = lax.broadcasted_iota(jnp.int32, (ROWS, 2 * ROWS), 0)
+    wide_column = lax.broadcasted_iota(jnp.int32, (ROWS, 2 * ROWS), 1)
+    for h in range(2):
+        source = (wide_row // PORTION) * 8 + h * PORTION + lax.rem(wide_row, PORTION)
+        select = (wide_column == source).astype(jnp.float32).astype(jnp.bfloat16)
+        heads[:, h * (WIDTH // 2) : (h + 1) * (WIDTH // 2)] = jnp.dot(
+            select, heads_ref[...], preferred_element_type=jnp.float32
+        ).astype(jnp.bfloat16)
+
     def product(n, c):
         return jnp.dot(
-            heads_ref[...], wo[n, :, c * CW : (c + 1) * CW], preferred_element_type=jnp.float32
+            heads[...], wo[n, :, c * CW : (c + 1) * CW], preferred_element_type=jnp.float32
         )
 
     def remote(n, src, dst, target):
@@ -590,9 +661,10 @@
     return pl.pallas_call(
         output_kernel,
         out_shape=jax.ShapeDtypeStruct((ROWS, WIDTH), bf16),
-        in_specs=[vmem, vmem, pl.BlockSpec(memory_space=pl.ANY)],
+        in_specs=[vmem, vmem, pl.BlockSpec(memory_space=pltpu.HBM)],
         out_specs=vmem,
         scratch_shapes=[
+            pltpu.VMEM((ROWS, WIDTH), bf16),
             pltpu.VMEM((TP, WIDTH, WIDTH), bf16),
             pltpu.VMEM((CHUNKS, ROWS, CW), bf16),
             pltpu.VMEM((CHUNKS, 2, ROWS, CW), bf16),
@@ -617,14 +689,19 @@
     slot_rows = (slots[:, None] * PORTION + jnp.arange(PORTION, dtype=jnp.int32)[None, :]).reshape(
         1, ROWS
     )
-    keys, values, queries = gather_call(
+    hidden, query_weight, key_matrix, value_matrix, output_weight = (
+        pltpu.with_memory_space_constraint(a, pltpu.HBM)
+        for a in (hidden, query_weight, key_matrix, value_matrix, output_weight)
+    )
+    keys, values, queries, marks = gather_call(
         bounds, hidden, query_weight, key_matrix, value_matrix, inverse
     )
     heads = attend_call(
         bounds,
-        queries.reshape(ROWS, WIDTH),
+        queries.reshape(2 * ROWS, WIDTH // 2),
         keys.reshape(TOKENS, HEAD),
         values.reshape(TOKENS, HEAD),
+        marks,
     )
     return output_call(slot_rows, heads, output_weight)
 

time: 131 us -> 113 us (0.86); the launches traced: 134 us -> 112 us
  Pallas kernels: 122 us -> 110 us
  local copies, waits for them, and re-layouts: 11.6 us -> 1.58 us
    unnamed x17 -> x5, local copies, waits for them, and re-layouts: 11.5 us -> 1.46 us
    pallas_call x1, Pallas kernels: 27.3 us -> 18.3 us  [attend_call(): pl.pallas_call(attend_kernel, out_shape=jax.ShapeDtypeStruct((2 * ROWS, W...]
    pallas_call x1, Pallas kernels: 35.1 us -> 33.3 us  [output_call(): pl.pallas_call(output_kernel, out_shape=jax.ShapeDtypeStruct((ROWS, WIDTH...]
where the time goes in v1:
time: 113 us; the launch traced here: 112 us
  Pallas kernels  110 us (97%)
  local copies, waits for them, and re-layouts  1.58 us (1%)
    pallas_call x1, Pallas kernels, gather_call(): pl.pallas_call(gather_kernel, out_shape=(kv, kv, jax.ShapeDtypeStruct((CP...  58.6 us
    pallas_call x1, Pallas kernels, output_call(): pl.pallas_call(output_kernel, out_shape=jax.ShapeDtypeStruct((ROWS, WIDTH...  33.3 us
    pallas_call x1, Pallas kernels, attend_call(): pl.pallas_call(attend_kernel, out_shape=jax.ShapeDtypeStruct((2 * ROWS, W...  18.3 us

profile of v1, /device:TPU:1, one launch (start us, length us, event | category | flops | bytes accessed | tf_op | source)
XLA Modules:
  0.0 112.2 jit_solution(9563794760627765116)
XLA Ops:
  0.0 0.1 maximum_bitcast_fusion.inverse_ref
  0.1 0.0 copy-start
  0.1 0.7 copy-done
  0.8 58.6 %gather_project.1 = (bf16[4,4,2,4,64,128]{5,4,3,2,1,0:T(8,128)(2,1)S(1)}, bf16[4,4,2,4,64,128]{5,4,3,2,1,0:T(8,128)(2,1)S(1)}, bf16[32,2,8,512]{3,2,1,0:T(8,128)(2,1)S(1)}, bf16[8192,128]{1,0:T(8,128)(2,1)S(1)}) custom-call(s32[9]{0:T(128)S(1)} %copy-done, bf16[256,1024]{1,0:T(8,128)(2,1)} %hidden_ref.1, bf16[4096,1024]{1,0:T(8,128)(2,1)} %wq_ref.1, ...), custom_call_target="tpu_custom_call" | custom-call | tf_op jit(solution)/shard_map/gather_project/pallas_call | solution.py:382
  59.4 0.0 copy-start.1
  59.4 18.3 %attend.1.heads_ref = bf16[512,512]{1,0:T(8,128)(2,1)S(1)} custom-call(s32[9]{0:T(128)S(1)} %copy-done, bf16[512,512]{1,0:T(8,128)(2,1)S(1)} %bitcast.7, bf16[8192,128]{1,0:T(8,128)(2,1)S(1)} %bitcast.5, bf16[8192,128]{1,0:T(8,128)(2,1)S(1)} %bitcast.6, bf16[8192,128]{1,0:T(8,128)(2,1)S(1)} %get-tuple-element.12.mark_ref), custom_call_target="tpu_custom_call" | custom-call | tf_op jit(solution)/shard_map/attend/pallas_call | solution.py:481
  77.7 0.0 copy-done.1
  77.7 0.2 convert_reduce_fusion
  77.9 0.1 iota_add_fusion
  77.9 0.1 add.36.slot_ref
  78.1 33.3 %project_out.1 = bf16[256,1024]{1,0:T(8,128)(2,1)S(1)} custom-call(s32[1,256]{1,0:T(1,128)S(1)} %add.36.slot_ref, bf16[512,512]{1,0:T(8,128)(2,1)S(1)} %attend.1.heads_ref, bf16[1024,4096]{1,0:T(8,128)(2,1)} %wo_ref.1), custom_call_target="tpu_custom_call" | custom-call | tf_op jit(solution)/shard_map/project_out/pallas_call | solution.py:661
  111.4 0.8 copy.9
  (2 shorter events, 0.0 us)
Async XLA Ops:
  0.1 0.7 copy-start
  59.4 18.3 %copy-start.1 = (s32[64]{0:T(128)S(1)}, s32[64]{0:T(128)}, u32[]{:S(2)}) copy-start(s32[64]{0:T(128)} %param.13) | copy-start | bytes 772

commit v2 on v1

--- a/solution.py
+++ b/solution.py
@@ -54,6 +54,7 @@
 
 PARTS = 4
 PART = ROWS // PARTS
+RELAYED = 2
 SPAN = 8
 PENALTY = -1e30
 
@@ -219,12 +220,15 @@
         a_next, a_prev = lax.rem(a + 1, 4), lax.rem(a + 3, 4)
         b_next, b_prev = lax.rem(b + 1, 4), lax.rem(b + 3, 4)
         b_far = lax.rem(b + 2, 4)
+        direct = r >= RELAYED
         return dict(
             ring1=(
                 copy(0, piece(a, 0, PART), neighbour(0, 1)),
                 copy(1, piece(a, 0, PART), neighbour(0, 3)),
             ),
-            ring1_far=(
+            ring1_far=(copy(2, piece(a, 0, PART), neighbour(0, 2)),)
+            if direct
+            else (
                 copy(2, piece(a_prev, 0, half), neighbour(0, 1)),
                 copy(3, piece(a_next, half, half), neighbour(0, 3)),
             ),
@@ -232,7 +236,9 @@
                 copy(4, line(b, 0, 4), neighbour(1, 1)),
                 copy(5, line(b, 0, 4), neighbour(1, 3)),
             ),
-            ring2_far=(
+            ring2_far=(copy(6, line(b, 0, 4), neighbour(1, 2)),)
+            if direct
+            else (
                 copy(6, line(b_prev, 0, 2), neighbour(1, 1)),
                 copy(7, line(b_next, 2, 2), neighbour(1, 3)),
             ),
@@ -272,19 +278,25 @@
         )
         v_ref[xcoord, ycoord, core, r] = raw[:, HEAD:].astype(jnp.bfloat16)
         start(r, "ring1")
+        if r >= RELAYED:
+            start(r, "ring1_far")
 
     def s1(r):
         arrived(r, "ring1")
-        start(r, "ring1_far")
+        if r < RELAYED:
+            start(r, "ring1_far")
 
     def s2(r):
         arrived(r, "ring1_far")
         start(r, "ring2")
+        if r >= RELAYED:
+            start(r, "ring2_far")
         across(r, (0,))
 
     def s3(r):
         arrived(r, "ring2")
-        start(r, "ring2_far")
+        if r < RELAYED:
+            start(r, "ring2_far")
         across(r, (1, 2))
 
     def s4(r):
@@ -330,36 +342,36 @@
     lax.fori_loop(NBLK // 2, NBLK, mark, 0)
     relay_z(1)
     s0(0)
+    relay_z(2)
     s1(0)
-    relay_z(2)
-    s2(0)
     s0(1)
     queries(0, 0)
     queries(0, 1)
+    s2(0)
+    relay_z(3)
     s1(1)
-    relay_z(3)
-    s3(0)
+    s0(2)
     queries(0, 2)
     s2(1)
-    s0(2)
+    s3(0)
     queries(0, 3)
+    s0(3)
     spread(0)
+    s1(2)
+    s2(2)
+    s1(3)
+    s2(3)
+    s3(1)
     s4(0)
-    s0(3)
-    s1(2)
-    s3(1)
     queries(1, 0)
-    s1(3)
-    s2(2)
     queries(1, 1)
     s4(1)
     queries(1, 2)
-    s2(3)
     queries(1, 3)
     spread(1)
     s3(2)
+    s4(2)
     s3(3)
-    s4(2)
     s4(3)
     spread_done(0)
     spread_done(1)
@@ -410,70 +422,130 @@
 TILE = SPAN * BLOCK
 
 
-def attend_kernel(bounds_ref, q_ref, k_ref, v_ref, mark_ref, o_ref):
+GROUPS = NBLK // SPAN
+QROWS = 4 * SPAN * 8
+
+
+def attend_kernel(
+    bounds_ref, q_ref, k_ref, v_ref, mark_ref, o_ref,
+    turned, asked, even, odd, mixed_ref, total_ref,
+):
     rows = SPAN * 8
-    count = 4 * rows
     factor = math.log2(math.e) / math.sqrt(HEAD)
-    row = lax.rem(lax.broadcasted_iota(jnp.int32, (count, HEAD), 0), rows)
-    lane = lax.broadcasted_iota(jnp.int32, (count, HEAD), 1)
+    row = lax.rem(lax.broadcasted_iota(jnp.int32, (rows, HEAD), 0), rows)
+    lane = lax.broadcasted_iota(jnp.int32, (rows, HEAD), 1)
     block, step = row // 8, lax.rem(row, PORTION)
     key_block, key_step = (lane - 8) // (PORTION + 1), lax.rem(lane - 8, PORTION + 1)
     later = (key_block > block) | ((key_block == block) & (key_step > step))
     later = later & (lane >= 8) & (lane < 8 + SPAN * (PORTION + 1))
     me = lax.axis_index("cp")
-    ones = jnp.ones((TILE, HEAD), jnp.bfloat16)
-
-    def group(g, carry):
-        first = pl.multiple_of(g * rows, rows)
+    contract_last = (((1,), (1,)), ((), ()))
+    diagonal = lax.broadcasted_iota(jnp.int32, (HEAD, HEAD), 0) == lax.broadcasted_iota(
+        jnp.int32, (HEAD, HEAD), 1
+    )
+    identity = diagonal.astype(jnp.float32).astype(jnp.bfloat16)
+
+    def prepare(g, carry):
+        at = pl.ds(pl.multiple_of(g * TILE, TILE), TILE)
+        turned[:, at] = lax.dot_general(
+            identity, v_ref[at, :], contract_last, preferred_element_type=jnp.float32
+        ).astype(jnp.bfloat16)
         tokens = (g * SPAN + block) * BLOCK + me * PORTION + step
         document = jnp.zeros_like(tokens)
+        for i in range(1, 8):
+            document = jnp.where(tokens >= bounds_ref[i], i, document)
+        other = (lane < 8) & (lane != document)
+        inner = jnp.where(other, PENALTY, 0.0).astype(jnp.bfloat16)
+        outer = jnp.where(other | later, PENALTY, 0.0).astype(jnp.bfloat16)
+        first = pl.multiple_of(g * rows, rows)
+        for h in range(4):
+            part = q_ref[pl.ds(first, rows), h * HEAD : (h + 1) * HEAD]
+            for n, penalties in enumerate((inner, outer)):
+                asked[2 * g + n, h * rows : (h + 1) * rows, :HEAD] = part
+                asked[2 * g + n, h * rows : (h + 1) * rows, HEAD:] = penalties
+        return carry
+
+    lax.fori_loop(0, GROUPS, prepare, 0)
+
+    def lowest(g):
         low = jnp.int32(0)
         for i in range(1, 8):
-            document = jnp.where(tokens >= bounds_ref[i], i, document)
             low = jnp.where(g * TILE >= bounds_ref[i], bounds_ref[i], low)
-        other = (lane < 8) & (lane != document)
-        q = jnp.concatenate(
-            [q_ref[pl.ds(first, rows), h * HEAD : (h + 1) * HEAD] for h in range(4)], axis=0
-        )
-        inner = jnp.where(other, PENALTY, 0.0).astype(jnp.bfloat16)
-        outer = jnp.where(other | later, PENALTY, 0.0).astype(jnp.bfloat16)
-
-        def scores_of(j, penalties):
-            at = pl.ds(pl.multiple_of(j * TILE, TILE), TILE)
-            return lax.dot_general(
-                jnp.concatenate([q, penalties], axis=1),
+        return low // TILE
+
+    def following(item):
+        g, j = item
+        more = j > lowest(g)
+        return jnp.where(more, g, g + 1), jnp.where(more, j - 1, g + 1)
+
+    def score(item, ref):
+        g, j = item
+        own = jnp.where(g == j, 1, 0)
+        q = asked[2 * jnp.minimum(g, GROUPS - 1) + own]
+        for part in range(2):
+            size = TILE // 2
+            first = jnp.minimum(j, GROUPS - 1) * TILE + part * size
+            at = pl.ds(pl.multiple_of(first, size), size)
+            ref[part * size : (part + 1) * size, :] = lax.dot_general(
                 jnp.concatenate([k_ref[at, :], mark_ref[at, :]], axis=1),
-                (((1,), (1,)), ((), ())),
-                preferred_element_type=jnp.float32,
-            ) * factor
-
-        def mix(j, scores, top):
-            at = pl.ds(pl.multiple_of(j * TILE, TILE), TILE)
-            weights = jnp.exp2(scores - top).astype(jnp.bfloat16)
-            return jnp.dot(
-                weights,
-                jnp.concatenate([v_ref[at, :], ones], axis=1),
+                q,
+                contract_last,
                 preferred_element_type=jnp.float32,
             )
 
-        scores = scores_of(g, outer)
-        top = jnp.max(scores, axis=1, keepdims=True)
-        mixed = mix(g, scores, top)
-
-        def tile(n, state):
-            top, mixed = state
-            j = g - 1 - n
-            scores = scores_of(j, inner)
-            new_top = jnp.maximum(top, jnp.max(scores, axis=1, keepdims=True))
-            return new_top, mixed * jnp.exp2(top - new_top) + mix(j, scores, new_top)
-
-        top, mixed = lax.fori_loop(0, g - low // TILE, tile, (top, mixed))
-        out = (mixed[:, :HEAD] / mixed[:, HEAD:]).astype(jnp.bfloat16)
+    def soften(item, ref, state):
+        g, j = item
+        top, total, mixed = state
+        top = jnp.where(g == j, 0.5 * PENALTY, top)
+        at = pl.ds(pl.multiple_of(jnp.minimum(j, GROUPS - 1) * TILE, TILE), TILE)
+        new_top = jnp.maximum(top, jnp.max(ref[...], axis=0, keepdims=True))
+        shrink = jnp.exp2((top - new_top) * factor)
+        weights = jnp.exp2((ref[...] - new_top) * factor)
+        total = total * shrink + jnp.sum(weights, axis=0, keepdims=True)
+        mixed = mixed * shrink + jnp.dot(
+            turned[:, at], weights.astype(jnp.bfloat16), preferred_element_type=jnp.float32
+        )
+        mixed_ref[g] = mixed
+        total_ref[g] = total
+        return new_top, total, mixed
+
+    count = lax.fori_loop(0, GROUPS, lambda g, n: n + g + 1 - lowest(g), jnp.int32(0))
+    zero = jnp.int32(0)
+    score((zero, zero), even)
+
+    def pair(n, carry):
+        g, j, *state = carry
+        item = (g, j)
+        second = following(item)
+        score(second, odd)
+        state = soften(item, even, state)
+        third = following(second)
+        third = (jnp.minimum(third[0], GROUPS), jnp.minimum(third[1], GROUPS))
+        score(third, even)
+        state = soften(second, odd, state)
+        return (*third, *state)
+
+    lax.fori_loop(
+        0,
+        (count + 1) // 2,
+        pair,
+        (
+            zero,
+            zero,
+            jnp.full((1, QROWS), 0.5 * PENALTY, jnp.float32),
+            jnp.zeros((1, QROWS), jnp.float32),
+            jnp.zeros((HEAD, QROWS), jnp.float32),
+        ),
+    )
+
+    def finish(g, carry):
+        out = (mixed_ref[g] / total_ref[g]).T.astype(jnp.bfloat16)
+        first = pl.multiple_of(g * rows, rows)
         for h in range(4):
             o_ref[pl.ds(first, rows), h * HEAD : (h + 1) * HEAD] = out[h * rows : (h + 1) * rows]
         return carry
 
-    lax.fori_loop(0, NBLK // SPAN, group, 0)
+    lax.fori_loop(0, GROUPS, finish, 0)
 
 
 def attend_call(bounds, q, k, v, marks):
@@ -483,7 +555,15 @@
         out_shape=jax.ShapeDtypeStruct((2 * ROWS, WIDTH // 2), jnp.bfloat16),
         in_specs=[pl.BlockSpec(memory_space=pltpu.SMEM), vmem, vmem, vmem, vmem],
         out_specs=vmem,
-        compiler_params=pltpu.CompilerParams(vmem_limit_bytes=20 * 1024 * 1024),
+        scratch_shapes=[
+            pltpu.VMEM((HEAD, TOKENS), jnp.bfloat16),
+            pltpu.VMEM((2 * GROUPS, QROWS, 2 * HEAD), jnp.bfloat16),
+            pltpu.VMEM((TILE, QROWS), jnp.float32),
+            pltpu.VMEM((TILE, QROWS), jnp.float32),
+            pltpu.VMEM((GROUPS + 1, HEAD, QROWS), jnp.float32),
+            pltpu.VMEM((GROUPS + 1, 1, QROWS), jnp.float32),
+        ],
+        compiler_params=pltpu.CompilerParams(vmem_limit_bytes=28 * 1024 * 1024),
         name="attend",
     )(bounds, q, k, v, marks)
 

time: 113 us -> 106 us (0.938)
  Pallas kernels: 110 us -> 103 us
    pallas_call x1, Pallas kernels: 18.3 us -> 12 us  [attend_call(): pl.pallas_call(attend_kernel, out_shape=jax.ShapeDtypeStruct((2 * ROWS, W...]
    pallas_call x1, Pallas kernels: 58.6 us -> 54.8 us  [gather_call(): pl.pallas_call(gather_kernel, out_shape=(kv, kv, jax.ShapeDtypeStruct((CP...]
    pallas_call x1, Pallas kernels: 33.3 us -> 36.2 us  [output_call(): pl.pallas_call(output_kernel, out_shape=jax.ShapeDtypeStruct((ROWS, WIDTH...]
where the time goes in v2:
time: 106 us; the launch traced here: 105 us
  Pallas kernels  103 us (97%)
  local copies, waits for them, and re-layouts  1.58 us (1%)
    pallas_call x1, Pallas kernels, gather_call(): pl.pallas_call(gather_kernel, out_shape=(kv, kv, jax.ShapeDtypeStruct((CP...  54.8 us
    pallas_call x1, Pallas kernels, output_call(): pl.pallas_call(output_kernel, out_shape=jax.ShapeDtypeStruct((ROWS, WIDTH...  36.2 us
    pallas_call x1, Pallas kernels, attend_call(): pl.pallas_call(attend_kernel, out_shape=jax.ShapeDtypeStruct((2 * ROWS, W...  12 us

profile of v2, /device:TPU:1, one launch (start us, length us, event | category | flops | bytes accessed | tf_op | source)
XLA Modules:
  0.0 104.9 jit_solution(14201416926570254653)
XLA Ops:
  0.0 0.1 maximum_bitcast_fusion.inverse_ref
  0.1 0.0 copy-start
  0.1 0.7 copy-done
  0.8 54.8 %gather_project.1 = (bf16[4,4,2,4,64,128]{5,4,3,2,1,0:T(8,128)(2,1)S(1)}, bf16[4,4,2,4,64,128]{5,4,3,2,1,0:T(8,128)(2,1)S(1)}, bf16[32,2,8,512]{3,2,1,0:T(8,128)(2,1)S(1)}, bf16[8192,128]{1,0:T(8,128)(2,1)S(1)}) custom-call(s32[9]{0:T(128)S(1)} %copy-done, bf16[256,1024]{1,0:T(8,128)(2,1)} %hidden_ref.1, bf16[4096,1024]{1,0:T(8,128)(2,1)} %wq_ref.1, ...), custom_call_target="tpu_custom_call" | custom-call | tf_op jit(solution)/shard_map/gather_project/pallas_call | solution.py:394
  55.5 0.0 copy-start.1
  55.6 12.0 %attend.1.heads_ref = bf16[512,512]{1,0:T(8,128)(2,1)S(1)} custom-call(s32[9]{0:T(128)S(1)} %copy-done, bf16[512,512]{1,0:T(8,128)(2,1)S(1)} %bitcast.7, bf16[8192,128]{1,0:T(8,128)(2,1)S(1)} %bitcast.5, bf16[8192,128]{1,0:T(8,128)(2,1)S(1)} %bitcast.6, bf16[8192,128]{1,0:T(8,128)(2,1)S(1)} %get-tuple-element.12.mark_ref), custom_call_target="tpu_custom_call" | custom-call | tf_op jit(solution)/shard_map/attend/pallas_call | solution.py:553
  67.5 0.0 copy-done.1
  67.5 0.2 convert_reduce_fusion
  67.7 0.1 iota_add_fusion
  67.8 0.1 add.36.slot_ref
  67.9 36.2 %project_out.1 = bf16[256,1024]{1,0:T(8,128)(2,1)S(1)} custom-call(s32[1,256]{1,0:T(1,128)S(1)} %add.36.slot_ref, bf16[512,512]{1,0:T(8,128)(2,1)S(1)} %attend.1.heads_ref, bf16[1024,4096]{1,0:T(8,128)(2,1)} %wo_ref.1), custom_call_target="tpu_custom_call" | custom-call | tf_op jit(solution)/shard_map/project_out/pallas_call | solution.py:741
  104.1 0.8 copy.9
  (2 shorter events, 0.0 us)
Async XLA Ops:
  0.1 0.7 copy-start
  55.5 12.0 %copy-start.1 = (s32[64]{0:T(128)S(1)}, s32[64]{0:T(128)}, u32[]{:S(2)}) copy-start(s32[64]{0:T(128)} %param.13) | copy-start | bytes 772

commit v3 on v2

--- a/solution.py
+++ b/solution.py
@@ -52,9 +52,11 @@
     return start
 
 
-PARTS = 4
-PART = ROWS // PARTS
-RELAYED = 2
+SIZES = (64, 64, 64, 32, 32)
+STARTS = (0, 64, 128, 192, 224)
+PARTS = len(SIZES)
+STRAIGHT1 = (True, False, True, True, True)
+STRAIGHT2 = (True, False, False, False, True)
 SPAN = 8
 PENALTY = -1e30
 
@@ -110,18 +112,17 @@
             device_id_type=MESH,
         )
 
-    half = PART // 2
     own = [
         (
-            zcopy(4 * r, up, tp, r * PART, PART),
-            zcopy(4 * r + 1, down, tp, r * PART, PART),
+            zcopy(4 * r, up, tp, STARTS[r], SIZES[r]),
+            zcopy(4 * r + 1, down, tp, STARTS[r], SIZES[r]),
         )
         for r in range(PARTS)
     ]
     fwd = [
         (
-            zcopy(4 * r + 2, down, up, r * PART, half),
-            zcopy(4 * r + 3, up, down, r * PART + half, half),
+            zcopy(4 * r + 2, down, up, STARTS[r], SIZES[r] // 2),
+            zcopy(4 * r + 3, up, down, STARTS[r] + SIZES[r] // 2, SIZES[r] // 2),
         )
         for r in range(PARTS)
     ]
@@ -206,28 +207,28 @@
             )
 
         def piece(at, row, count):
-            rows = pl.ds(row, count)
+            rows = pl.ds(STARTS[r] + row, count)
             if which == 0:
-                return buffer.at[at, b, core, r, rows]
-            return buffer.at[b, at, core, r, rows]
+                return buffer.at[at, b, core, rows]
+            return buffer.at[b, at, core, rows]
 
         def line(at, first, count):
-            along = pl.ds(first, count)
+            along, rows = pl.ds(first, count), pl.ds(STARTS[r], SIZES[r])
             if which == 0:
-                return buffer.at[along, at, core, r]
-            return buffer.at[at, along, core, r]
+                return buffer.at[along, at, core, rows]
+            return buffer.at[at, along, core, rows]
 
         a_next, a_prev = lax.rem(a + 1, 4), lax.rem(a + 3, 4)
         b_next, b_prev = lax.rem(b + 1, 4), lax.rem(b + 3, 4)
         b_far = lax.rem(b + 2, 4)
-        direct = r >= RELAYED
+        size, half = SIZES[r], SIZES[r] // 2
         return dict(
             ring1=(
-                copy(0, piece(a, 0, PART), neighbour(0, 1)),
-                copy(1, piece(a, 0, PART), neighbour(0, 3)),
+                copy(0, piece(a, 0, size), neighbour(0, 1)),
+                copy(1, piece(a, 0, size), neighbour(0, 3)),
             ),
-            ring1_far=(copy(2, piece(a, 0, PART), neighbour(0, 2)),)
-            if direct
+            ring1_far=(copy(2, piece(a, 0, size), neighbour(0, 2)),)
+            if STRAIGHT1[r]
             else (
                 copy(2, piece(a_prev, 0, half), neighbour(0, 1)),
                 copy(3, piece(a_next, half, half), neighbour(0, 3)),
@@ -237,7 +238,7 @@
                 copy(5, line(b, 0, 4), neighbour(1, 3)),
             ),
             ring2_far=(copy(6, line(b, 0, 4), neighbour(1, 2)),)
-            if direct
+            if STRAIGHT2[r]
             else (
                 copy(6, line(b_prev, 0, 2), neighbour(1, 1)),
                 copy(7, line(b_next, 2, 2), neighbour(1, 3)),
@@ -270,32 +271,31 @@
     def s0(r):
         for copy in fwd[r]:
             copy.wait_recv()
-        raw = jnp.dot(
-            full[pl.ds(r * PART, PART), :], wkv[...], preferred_element_type=jnp.float32
-        )
-        k_ref[xcoord, ycoord, core, r] = rotate(raw[:, :HEAD], r * PART, PART).astype(
+        rows = pl.ds(STARTS[r], SIZES[r])
+        raw = jnp.dot(full[rows, :], wkv[...], preferred_element_type=jnp.float32)
+        k_ref[xcoord, ycoord, core, rows] = rotate(raw[:, :HEAD], STARTS[r], SIZES[r]).astype(
             jnp.bfloat16
         )
-        v_ref[xcoord, ycoord, core, r] = raw[:, HEAD:].astype(jnp.bfloat16)
+        v_ref[xcoord, ycoord, core, rows] = raw[:, HEAD:].astype(jnp.bfloat16)
         start(r, "ring1")
-        if r >= RELAYED:
+        if STRAIGHT1[r]:
             start(r, "ring1_far")
 
     def s1(r):
         arrived(r, "ring1")
-        if r < RELAYED:
+        if not STRAIGHT1[r]:
             start(r, "ring1_far")
 
     def s2(r):
         arrived(r, "ring1_far")
         start(r, "ring2")
-        if r >= RELAYED:
+        if STRAIGHT2[r]:
             start(r, "ring2_far")
         across(r, (0,))
 
     def s3(r):
         arrived(r, "ring2")
-        if r < RELAYED:
+        if not STRAIGHT2[r]:
             start(r, "ring2_far")
         across(r, (1, 2))
 
@@ -345,33 +345,39 @@
     relay_z(2)
     s1(0)
     s0(1)
+    s2(0)
     queries(0, 0)
     queries(0, 1)
-    s2(0)
     relay_z(3)
+    queries(0, 2)
+    queries(0, 3)
+    s0(2)
     s1(1)
-    s0(2)
-    queries(0, 2)
+    spread(0)
+    relay_z(4)
+    s0(3)
+    s3(0)
+    s1(2)
     s2(1)
-    s3(0)
-    queries(0, 3)
-    s0(3)
-    spread(0)
-    s1(2)
+    s4(0)
+    s0(4)
     s2(2)
+    queries(1, 0)
+    queries(1, 1)
+    queries(1, 2)
+    queries(1, 3)
     s1(3)
+    spread(1)
     s2(3)
     s3(1)
-    s4(0)
-    queries(1, 0)
-    queries(1, 1)
+    s1(4)
+    s2(4)
+    s3(2)
+    s3(3)
     s4(1)
-    queries(1, 2)
-    queries(1, 3)
-    spread(1)
-    s3(2)
+    s3(4)
     s4(2)
-    s3(3)
+    s4(4)
     s4(3)
     spread_done(0)
     spread_done(1)
@@ -389,7 +395,7 @@
 def gather_call(bounds, hidden, wq, wk, wv, inverse):
     vmem = pl.BlockSpec(memory_space=pltpu.VMEM)
     hbm = pl.BlockSpec(memory_space=pltpu.HBM)
-    kv = jax.ShapeDtypeStruct((4, 4, 2, PARTS, PART, HEAD), jnp.bfloat16)
+    kv = jax.ShapeDtypeStruct((4, 4, 2, ROWS, HEAD), jnp.bfloat16)
     dma = pltpu.SemaphoreType.DMA
     return pl.pallas_call(
         gather_kernel,
@@ -424,6 +430,7 @@
 
 GROUPS = NBLK // SPAN
 QROWS = 4 * SPAN * 8
+PIECE = 256
 
 
 def attend_kernel(
@@ -497,14 +504,17 @@
         g, j = item
         top, total, mixed = state
         top = jnp.where(g == j, 0.5 * PENALTY, top)
-        at = pl.ds(pl.multiple_of(jnp.minimum(j, GROUPS - 1) * TILE, TILE), TILE)
+        start = jnp.minimum(j, GROUPS - 1) * TILE
         new_top = jnp.maximum(top, jnp.max(ref[...], axis=0, keepdims=True))
         shrink = jnp.exp2((top - new_top) * factor)
-        weights = jnp.exp2((ref[...] - new_top) * factor)
-        total = total * shrink + jnp.sum(weights, axis=0, keepdims=True)
-        mixed = mixed * shrink + jnp.dot(
-            turned[:, at], weights.astype(jnp.bfloat16), preferred_element_type=jnp.float32
-        )
+        total, mixed = total * shrink, mixed * shrink
+        for first in range(0, TILE, PIECE):
+            weights = jnp.exp2((ref[first : first + PIECE, :] - new_top) * factor)
+            total = total + jnp.sum(weights, axis=0, keepdims=True)
+            keys = pl.ds(pl.multiple_of(start + first, PIECE), PIECE)
+            mixed = mixed + jnp.dot(
+                turned[:, keys], weights.astype(jnp.bfloat16), preferred_element_type=jnp.float32
+            )
         mixed_ref[g] = mixed
         total_ref[g] = total
         return new_top, total, mixed
@@ -568,8 +578,9 @@
     )(bounds, q, k, v, marks)
 
 
-CHUNKS = 4
-CW = WIDTH // CHUNKS
+CHUNKS = (2, 2, 2, 1, 1)
+FIRST = (0, 2, 4, 6, 7)
+PIECES = WIDTH // HEAD
 
 
 def output_kernel(
@@ -609,9 +620,8 @@
         ).astype(jnp.bfloat16)
 
     def product(n, c):
-        return jnp.dot(
-            heads[...], wo[n, :, c * CW : (c + 1) * CW], preferred_element_type=jnp.float32
-        )
+        columns = slice(FIRST[c] * HEAD, (FIRST[c] + CHUNKS[c]) * HEAD)
+        return jnp.dot(heads[...], wo[n, :, columns], preferred_element_type=jnp.float32)
 
     def remote(n, src, dst, target):
         return pltpu.make_async_remote_copy(
@@ -624,38 +634,57 @@
         )
 
     half = ROWS // 2
+    upper, lower = pl.ds(0, half), pl.ds(half, half)
     far_copies, near_copies = [], []
-    for c in range(CHUNKS):
+    for c, count in enumerate(CHUNKS):
+        at = pl.ds(FIRST[c], count)
         far_copies.append(
             (
-                remote(4 * c, far.at[c, pl.ds(0, half)], far_in.at[c, 0], up),
-                remote(4 * c + 1, far.at[c, pl.ds(half, half)], far_in.at[c, 1], down),
+                remote(4 * c, far.at[0, at], far_in.at[0, at], up),
+                remote(4 * c + 1, far.at[1, at], far_in.at[1, at], down),
             )
         )
         near_copies.append(
             (
-                remote(4 * c + 2, near.at[c, 0], near_in.at[c, 0], up),
-                remote(4 * c + 3, near.at[c, 1], near_in.at[c, 1], down),
+                remote(4 * c + 2, near.at[0, at], near_in.at[0, at], up),
+                remote(4 * c + 3, near.at[1, at], near_in.at[1, at], down),
             )
         )
 
+    def pieces(c):
+        return [(FIRST[c] + n, slice(n * HEAD, (n + 1) * HEAD)) for n in range(CHUNKS[c])]
+
+    def make_far(c):
+        value = product(0, c).astype(jnp.bfloat16)
+        for at, columns in pieces(c):
+            far[0, at] = value[:half, columns]
+            far[1, at] = value[half:, columns]
+
     def send_far(c):
-        far[c] = product(0, c).astype(jnp.bfloat16)
         for copy in far_copies[c]:
             copy.start()
 
     def send_near(c):
         to_up, to_down = product(1, c), product(2, c)
         far_copies[c][0].wait_recv()
-        near[c, 0, :half] = (to_up[:half] + far_in[c, 0].astype(jnp.float32)).astype(jnp.bfloat16)
-        near[c, 0, half:] = to_up[half:].astype(jnp.bfloat16)
+        for at, columns in pieces(c):
+            near[0, at, upper] = (
+                to_up[:half, columns] + far_in[0, at].astype(jnp.float32)
+            ).astype(jnp.bfloat16)
+            near[0, at, lower] = to_up[half:, columns].astype(jnp.bfloat16)
         near_copies[c][0].start()
         far_copies[c][1].wait_recv()
-        near[c, 1, :half] = to_down[:half].astype(jnp.bfloat16)
-        near[c, 1, half:] = (to_down[half:] + far_in[c, 1].astype(jnp.float32)).astype(
-            jnp.bfloat16
-        )
+        for at, columns in pieces(c):
+            near[1, at, upper] = to_down[:half, columns].astype(jnp.bfloat16)
+            near[1, at, lower] = (
+                to_down[half:, columns] + far_in[1, at].astype(jnp.float32)
+            ).astype(jnp.bfloat16)
         near_copies[c][1].start()
+
+    def sum_own(c):
+        value = product(3, c)
+        for at, columns in pieces(c):
+            own_sum[at] = value[:, columns]
 
     row = lax.broadcasted_iota(jnp.int32, (ROWS, ROWS), 0)
     column = lax.broadcasted_iota(jnp.int32, (ROWS, ROWS), 1)
@@ -664,9 +693,10 @@
     to_place = (column == origin).astype(jnp.float32).astype(jnp.bfloat16)
 
     def acopy(c, k, target, slot):
+        at = pl.ds(FIRST[c], CHUNKS[c])
         return pltpu.make_async_remote_copy(
-            src_ref=spread.at[c, target],
-            dst_ref=landed.at[c, slot],
+            src_ref=spread.at[target, at],
+            dst_ref=landed.at[slot, at],
             send_sem=a_send.at[c, k],
             recv_sem=a_recv.at[c, k],
             device_id={"cp": target},
@@ -676,14 +706,21 @@
     def finish_sum(c):
         for copy in near_copies[c]:
             copy.wait_recv()
-        total = (
-            own_sum[c]
-            + near_in[c, 0].astype(jnp.float32)
-            + near_in[c, 1].astype(jnp.float32)
-        ).astype(jnp.bfloat16)
+        total = jnp.concatenate(
+            [
+                (
+                    own_sum[at]
+                    + near_in[0, at].astype(jnp.float32)
+                    + near_in[1, at].astype(jnp.float32)
+                ).astype(jnp.bfloat16)
+                for at, columns in pieces(c)
+            ],
+            axis=1,
+        )
         picked = jnp.dot(to_owner, total, preferred_element_type=jnp.float32)
-        spread[c] = picked.reshape(CP, 8, CW).astype(jnp.bfloat16)
-        landed[c, me] = spread[c, me]
+        for at, columns in pieces(c):
+            spread[:, at] = picked[:, columns].reshape(CP, 8, HEAD).astype(jnp.bfloat16)
+            landed[me, at] = spread[me, at]
 
         def send(k, carry):
             acopy(c, k, lax.rem(me + k, CP), me).start()
@@ -699,36 +736,47 @@
             return carry
 
         lax.fori_loop(1, CP, wait, 0)
-        rows = landed[c].astype(jnp.float32).reshape(ROWS, CW).astype(jnp.bfloat16)
-        out_ref[:, c * CW : (c + 1) * CW] = jnp.dot(
+        rows = jnp.concatenate(
+            [
+                landed[:, at].astype(jnp.float32).reshape(ROWS, HEAD).astype(jnp.bfloat16)
+                for at, columns in pieces(c)
+            ],
+            axis=1,
+        )
+        out_ref[:, FIRST[c] * HEAD : (FIRST[c] + CHUNKS[c]) * HEAD] = jnp.dot(
             to_place, rows, preferred_element_type=jnp.float32
         ).astype(jnp.bfloat16)
 
     loads[0].wait()
-    far[0] = product(0, 0).astype(jnp.bfloat16)
+    make_far(0)
     pl.semaphore_wait(barrier, CP + 1)
-    for copy in far_copies[0]:
-        copy.start()
+    send_far(0)
+    make_far(1)
     send_far(1)
+    make_far(2)
+    send_far(2)
     loads[1].wait()
     loads[2].wait()
     send_near(0)
-    send_far(2)
+    make_far(3)
+    send_far(3)
     send_near(1)
-    send_far(3)
+    make_far(4)
+    send_far(4)
+    send_near(2)
     loads[3].wait()
-    own_sum[0] = product(3, 0)
-    send_near(2)
-    own_sum[1] = product(3, 1)
+    for c in range(len(CHUNKS)):
+        sum_own(c)
     send_near(3)
-    own_sum[2] = product(3, 2)
-    own_sum[3] = product(3, 3)
-    for c in range(CHUNKS):
-        finish_sum(c)
-        if c > 0:
-            place(c - 1)
-    place(CHUNKS - 1)
-    for c in range(CHUNKS):
+    finish_sum(0)
+    send_near(4)
+    finish_sum(1)
+    finish_sum(2)
+    finish_sum(3)
+    finish_sum(4)
+    for c in range(len(CHUNKS)):
+        place(c)
+    for c in range(len(CHUNKS)):
         for copy in (*far_copies[c], *near_copies[c]):
             copy.wait_send()
 
@@ -746,14 +794,15 @@
         scratch_shapes=[
             pltpu.VMEM((ROWS, WIDTH), bf16),
             pltpu.VMEM((TP, WIDTH, WIDTH), bf16),
-            pltpu.VMEM((CHUNKS, ROWS, CW), bf16),
-            pltpu.VMEM((CHUNKS, 2, ROWS, CW), bf16),
-            pltpu.VMEM((CHUNKS, 2, half, CW), bf16),
-            pltpu.VMEM((CHUNKS, 2, ROWS, CW), bf16),
-            pltpu.VMEM((CHUNKS, CP, 8, CW), bf16),
-            pltpu.VMEM((CHUNKS, CP, 8, CW), bf16),
-            pltpu.VMEM((CHUNKS, ROWS, CW), jnp.float32),
-            dma((4,)), dma((4 * CHUNKS,)), dma((4 * CHUNKS,)), dma((CHUNKS, CP)), dma((CHUNKS, CP)),
+            pltpu.VMEM((2, PIECES, half, HEAD), bf16),
+            pltpu.VMEM((2, PIECES, ROWS, HEAD), bf16),
+            pltpu.VMEM((2, PIECES, half, HEAD), bf16),
+            pltpu.VMEM((2, PIECES, ROWS, HEAD), bf16),
+            pltpu.VMEM((CP, PIECES, 8, HEAD), bf16),
+            pltpu.VMEM((CP, PIECES, 8, HEAD), bf16),
+            pltpu.VMEM((PIECES, ROWS, HEAD), jnp.float32),
+            dma((4,)), dma((4 * len(CHUNKS),)), dma((4 * len(CHUNKS),)),
+            dma((len(CHUNKS), CP)), dma((len(CHUNKS), CP)),
         ],
         compiler_params=pltpu.CompilerParams(
             collective_id=1, has_side_effects=True, vmem_limit_bytes=40 * 1024 * 1024

time: 106 us -> 96.4 us (0.909); the launches traced: 105 us -> 96.7 us
  Pallas kernels: 103 us -> 94.7 us
    pallas_call x1, Pallas kernels: 36.2 us -> 31.1 us  [output_call(): pl.pallas_call(output_kernel, out_shape=jax.ShapeDtypeStruct((ROWS, WIDTH...]
    pallas_call x1, Pallas kernels: 54.8 us -> 50.4 us  [gather_call(): pl.pallas_call(gather_kernel, out_shape=(kv, kv, jax.ShapeDtypeStruct((CP...]
    pallas_call x1, Pallas kernels: 12 us -> 13.2 us  [attend_call(): pl.pallas_call(attend_kernel, out_shape=jax.ShapeDtypeStruct((2 * ROWS, W...]
where the time goes in v3:
time: 96.4 us; the launch traced here: 96.7 us
  Pallas kernels  94.7 us (98%)
  local copies, waits for them, and re-layouts  1.58 us (2%)
    pallas_call x1, Pallas kernels, gather_call(): pl.pallas_call(gather_kernel, out_shape=(kv, kv, jax.ShapeDtypeStruct((CP...  50.4 us
    pallas_call x1, Pallas kernels, output_call(): pl.pallas_call(output_kernel, out_shape=jax.ShapeDtypeStruct((ROWS, WIDTH...  31.1 us
    pallas_call x1, Pallas kernels, attend_call(): pl.pallas_call(attend_kernel, out_shape=jax.ShapeDtypeStruct((2 * ROWS, W...  13.2 us

profile of v3, /device:TPU:1, one launch (start us, length us, event | category | flops | bytes accessed | tf_op | source)
XLA Modules:
  0.0 96.7 jit_solution(10442743753712173592)
XLA Ops:
  0.0 0.1 maximum_bitcast_fusion.inverse_ref
  0.1 0.0 copy-start
  0.1 0.7 copy-done
  0.8 50.4 %gather_project.1 = (bf16[4,4,2,256,128]{4,3,2,1,0:T(8,128)(2,1)S(1)}, bf16[4,4,2,256,128]{4,3,2,1,0:T(8,128)(2,1)S(1)}, bf16[32,2,8,512]{3,2,1,0:T(8,128)(2,1)S(1)}, bf16[8192,128]{1,0:T(8,128)(2,1)S(1)}) custom-call(s32[9]{0:T(128)S(1)} %copy-done, bf16[256,1024]{1,0:T(8,128)(2,1)} %hidden_ref.1, bf16[4096,1024]{1,0:T(8,128)(2,1)} %wq_ref.1, ...), custom_call_target="tpu_custom_call" | custom-call | tf_op jit(solution)/shard_map/gather_project/pallas_call | solution.py:400
  51.2 0.0 copy-start.1
  51.2 13.2 %attend.1.heads_ref = bf16[512,512]{1,0:T(8,128)(2,1)S(1)} custom-call(s32[9]{0:T(128)S(1)} %copy-done, bf16[512,512]{1,0:T(8,128)(2,1)S(1)} %bitcast.7, bf16[8192,128]{1,0:T(8,128)(2,1)S(1)} %bitcast.5, bf16[8192,128]{1,0:T(8,128)(2,1)S(1)} %bitcast.6, bf16[8192,128]{1,0:T(8,128)(2,1)S(1)} %get-tuple-element.12.mark_ref), custom_call_target="tpu_custom_call" | custom-call | tf_op jit(solution)/shard_map/attend/pallas_call | solution.py:563
  64.4 0.0 copy-done.1
  64.4 0.2 convert_reduce_fusion
  64.6 0.1 iota_add_fusion
  64.7 0.1 add.36.slot_ref
  64.8 31.1 %project_out.1 = bf16[256,1024]{1,0:T(8,128)(2,1)S(1)} custom-call(s32[1,256]{1,0:T(1,128)S(1)} %add.36.slot_ref, bf16[512,512]{1,0:T(8,128)(2,1)S(1)} %attend.1.heads_ref, bf16[1024,4096]{1,0:T(8,128)(2,1)} %wo_ref.1), custom_call_target="tpu_custom_call" | custom-call | tf_op jit(solution)/shard_map/project_out/pallas_call | solution.py:789
  95.9 0.8 copy.9
  (2 shorter events, 0.0 us)
Async XLA Ops:
  0.1 0.7 copy-start
  51.2 13.2 %copy-start.1 = (s32[64]{0:T(128)S(1)}, s32[64]{0:T(128)}, u32[]{:S(2)}) copy-start(s32[64]{0:T(128)} %param.13) | copy-start | bytes 772

commit v4 on v3

--- a/solution.py
+++ b/solution.py
@@ -62,10 +62,10 @@
 
 
 def gather_kernel(
-    bounds_ref, hidden_ref, wq_ref, wk_ref, wv_ref, inverse_ref,
+    bounds_hbm, hidden_ref, wq_ref, wk_ref, wv_ref, inverse_ref,
     k_ref, v_ref, q_ref, mark_ref,
     full, wq, wkv, qtmp, qsend, cosine, sine,
-    w_sem, z_send, z_recv, g_send, g_recv, q_send, q_recv,
+    w_sem, z_send, z_recv, g_send, g_recv, q_send, q_recv, bounds_ref, met,
 ):
     me = lax.axis_index("cp")
     tp = lax.axis_index("tp")
@@ -82,23 +82,25 @@
         pltpu.make_async_copy(wv_ref, wkv.at[:, pl.ds(HEAD, HEAD)], w_sem.at[1]),
         pltpu.make_async_copy(wq_ref, wq, w_sem.at[2]),
     ]
+    bring_bounds = pltpu.make_async_copy(bounds_hbm, bounds_ref, w_sem.at[4])
     bring.start()
+    bring_bounds.start()
     for copy in weights:
         copy.start()
 
     barrier = pltpu.get_barrier_semaphore()
 
-    def greet(k, carry):
-        pl.semaphore_signal(
-            barrier, inc=1, device_id={"cp": lax.rem(me + k, CP)}, device_id_type=MESH
-        )
-        return carry
-
+    def signal(semaphore, target):
+        pl.semaphore_signal(semaphore, inc=1, device_id={"cp": target}, device_id_type=MESH)
+
+    along_x = [(lax.rem(xcoord + n, 4) * 4 + ycoord) * 2 + core for n in (1, 2, 3)]
+    along_y = [(xcoord * 4 + lax.rem(ycoord + n, 4)) * 2 + core for n in (1, 2, 3)]
     pl.semaphore_signal(barrier, inc=1, device_id={"tp": up}, device_id_type=MESH)
     pl.semaphore_signal(barrier, inc=1, device_id={"tp": down}, device_id_type=MESH)
-    lax.fori_loop(1, CP, greet, 0)
+    for target in (*along_x, *along_y, partner):
+        signal(barrier, target)
     bring.wait()
-    pl.semaphore_wait(barrier, CP + 1)
+    pl.semaphore_wait(barrier, 9)
 
     def zcopy(n, target, owner, row, count):
         columns = pl.ds(pl.multiple_of(owner * WIDTH, WIDTH), WIDTH)
@@ -128,6 +130,9 @@
     ]
     for copy in (*own[0], *own[1]):
         copy.start()
+    for target in along_x:
+        signal(met.at[0], target)
+    bring_bounds.wait()
 
     def relay_z(r):
         for copy in own[r]:
@@ -308,12 +313,12 @@
     origin = lax.rem(out_row // 4, 2) * BLOCK + (out_row // 8) * 4 + lax.rem(out_row, 4)
     pick = (in_row == origin).astype(jnp.float32).astype(jnp.bfloat16)
 
-    def qcopy(r, k, target, slot):
+    def qcopy(r, target, slot):
         return pltpu.make_async_remote_copy(
             src_ref=qsend.at[r, target],
             dst_ref=q_ref.at[slot, r],
-            send_sem=q_send.at[r, k],
-            recv_sem=q_recv.at[r, k],
+            send_sem=q_send.at[r],
+            recv_sem=q_recv.at[r],
             device_id={"cp": target},
             device_id_type=MESH,
         )
@@ -324,23 +329,22 @@
         q_ref[me, r] = qsend[r, me]
 
         def send(k, carry):
-            qcopy(r, k, lax.rem(me + k, CP), me).start()
+            qcopy(r, lax.rem(me + k, CP), me).start()
             return carry
 
         lax.fori_loop(1, CP, send, 0)
 
     def spread_done(r):
-        def wait(k, carry):
-            copy = qcopy(r, k, lax.rem(me + k, CP), lax.rem(me + CP - k, CP))
-            copy.wait_send()
-            copy.wait_recv()
-            return carry
-
-        lax.fori_loop(1, CP, wait, 0)
+        sent, landed = qsend.at[r, pl.ds(0, CP - 1)], q_ref.at[pl.ds(0, CP - 1), r]
+        pltpu.make_async_copy(sent, sent, q_send.at[r]).wait()
+        pltpu.make_async_copy(landed, landed, q_recv.at[r]).wait()
 
     relay_z(0)
+    pl.semaphore_wait(met.at[0], 3)
+    signal(met.at[1], partner)
     lax.fori_loop(NBLK // 2, NBLK, mark, 0)
     relay_z(1)
+    pl.semaphore_wait(met.at[1], 1)
     s0(0)
     relay_z(2)
     s1(0)
@@ -405,7 +409,7 @@
             jax.ShapeDtypeStruct((CP, 2, 8, WIDTH // 2), jnp.bfloat16),
             jax.ShapeDtypeStruct((TOKENS, HEAD), jnp.bfloat16),
         ),
-        in_specs=[pl.BlockSpec(memory_space=pltpu.SMEM), hbm, hbm, hbm, hbm, vmem],
+        in_specs=[hbm, hbm, hbm, hbm, hbm, vmem],
         out_specs=(vmem, vmem, vmem, vmem),
         scratch_shapes=[
             pltpu.VMEM((ROWS, TP * WIDTH), jnp.bfloat16),
@@ -415,8 +419,9 @@
             pltpu.VMEM((2, CP, 8, WIDTH // 2), jnp.bfloat16),
             pltpu.VMEM((ROWS, HEAD), jnp.float32),
             pltpu.VMEM((ROWS, HEAD), jnp.float32),
-            dma((4,)), dma((4 * PARTS,)), dma((4 * PARTS,)),
-            dma((24 * PARTS,)), dma((24 * PARTS,)), dma((2, CP)), dma((2, CP)),
+            dma((5,)), dma((4 * PARTS,)), dma((4 * PARTS,)),
+            dma((24 * PARTS,)), dma((24 * PARTS,)), dma((2,)), dma((2,)),
+            pltpu.SMEM((9,), jnp.int32), pltpu.SemaphoreType.REGULAR((2,)),
         ],
         compiler_params=pltpu.CompilerParams(
             collective_id=0, has_side_effects=True, vmem_limit_bytes=32 * 1024 * 1024
@@ -435,7 +440,7 @@
 
 def attend_kernel(
     bounds_ref, q_ref, k_ref, v_ref, mark_ref, o_ref,
-    turned, asked, even, odd, mixed_ref, total_ref,
+    turned, penalty_ref, even, odd, mixed_ref, total_ref,
 ):
     rows = SPAN * 8
     factor = math.log2(math.e) / math.sqrt(HEAD)
@@ -462,14 +467,8 @@
         for i in range(1, 8):
             document = jnp.where(tokens >= bounds_ref[i], i, document)
         other = (lane < 8) & (lane != document)
-        inner = jnp.where(other, PENALTY, 0.0).astype(jnp.bfloat16)
-        outer = jnp.where(other | later, PENALTY, 0.0).astype(jnp.bfloat16)
-        first = pl.multiple_of(g * rows, rows)
-        for h in range(4):
-            part = q_ref[pl.ds(first, rows), h * HEAD : (h + 1) * HEAD]
-            for n, penalties in enumerate((inner, outer)):
-                asked[2 * g + n, h * rows : (h + 1) * rows, :HEAD] = part
-                asked[2 * g + n, h * rows : (h + 1) * rows, HEAD:] = penalties
+        penalty_ref[2 * g] = jnp.where(other, PENALTY, 0.0).astype(jnp.bfloat16)
+        penalty_ref[2 * g + 1] = jnp.where(other | later, PENALTY, 0.0).astype(jnp.bfloat16)
         return carry
 
     lax.fori_loop(0, GROUPS, prepare, 0)
@@ -488,28 +487,42 @@
     def score(item, ref):
         g, j = item
         own = jnp.where(g == j, 1, 0)
-        q = asked[2 * jnp.minimum(g, GROUPS - 1) + own]
+        held = jnp.minimum(g, GROUPS - 1)
+        penalties = penalty_ref[2 * held + own]
+        asking = pl.ds(pl.multiple_of(held * rows, rows), rows)
+        q = jnp.concatenate(
+            [
+                jnp.concatenate([q_ref[asking, h * HEAD : (h + 1) * HEAD], penalties], axis=1)
+                for h in range(4)
+            ],
+            axis=0,
+        )
         for part in range(2):
             size = TILE // 2
             first = jnp.minimum(j, GROUPS - 1) * TILE + part * size
             at = pl.ds(pl.multiple_of(first, size), size)
-            ref[part * size : (part + 1) * size, :] = lax.dot_general(
+            scores = lax.dot_general(
                 jnp.concatenate([k_ref[at, :], mark_ref[at, :]], axis=1),
                 q,
                 contract_last,
                 preferred_element_type=jnp.float32,
             )
-
-    def soften(item, ref, state):
+            ref[part * size : (part + 1) * size, :] = scores
+            top = jnp.max(scores, axis=0, keepdims=True)
+            largest = top if part == 0 else jnp.maximum(largest, top)
+        return largest
+
+    def soften(item, ref, largest, state):
         g, j = item
         top, total, mixed = state
         top = jnp.where(g == j, 0.5 * PENALTY, top)
         start = jnp.minimum(j, GROUPS - 1) * TILE
-        new_top = jnp.maximum(top, jnp.max(ref[...], axis=0, keepdims=True))
+        new_top = jnp.maximum(top, largest)
         shrink = jnp.exp2((top - new_top) * factor)
         total, mixed = total * shrink, mixed * shrink
         for first in range(0, TILE, PIECE):
-            weights = jnp.exp2((ref[first : first + PIECE, :] - new_top) * factor)
+            piece = slice(first, first + PIECE)
+            weights = jnp.exp2((ref[piece, :] - new_top) * factor)
             total = total + jnp.sum(weights, axis=0, keepdims=True)
             keys = pl.ds(pl.multiple_of(start + first, PIECE), PIECE)
             mixed = mixed + jnp.dot(
@@ -521,19 +534,19 @@
 
     count = lax.fori_loop(0, GROUPS, lambda g, n: n + g + 1 - lowest(g), jnp.int32(0))
     zero = jnp.int32(0)
-    score((zero, zero), even)
+    highest = score((zero, zero), even)
 
     def pair(n, carry):
-        g, j, *state = carry
+        g, j, largest, *state = carry
         item = (g, j)
         second = following(item)
-        score(second, odd)
-        state = soften(item, even, state)
+        second_largest = score(second, odd)
+        state = soften(item, even, largest, state)
         third = following(second)
         third = (jnp.minimum(third[0], GROUPS), jnp.minimum(third[1], GROUPS))
-        score(third, even)
-        state = soften(second, odd, state)
-        return (*third, *state)
+        largest = score(third, even)
+        state = soften(second, odd, second_largest, state)
+        return (*third, largest, *state)
 
     lax.fori_loop(
         0,
@@ -542,6 +555,7 @@
         (
             zero,
             zero,
+            highest,
             jnp.full((1, QROWS), 0.5 * PENALTY, jnp.float32),
             jnp.zeros((1, QROWS), jnp.float32),
             jnp.zeros((HEAD, QROWS), jnp.float32),
@@ -549,10 +563,7 @@
     )
 
     def finish(g, carry):
-        out = (mixed_ref[g] / total_ref[g]).T.astype(jnp.bfloat16)
-        first = pl.multiple_of(g * rows, rows)
-        for h in range(4):
-            o_ref[pl.ds(first, rows), h * HEAD : (h + 1) * HEAD] = out[h * rows : (h + 1) * rows]
+        o_ref[g] = (mixed_ref[g] / total_ref[g]).astype(jnp.bfloat16)
         return carry
 
     lax.fori_loop(0, GROUPS, finish, 0)
@@ -562,12 +573,12 @@
     vmem = pl.BlockSpec(memory_space=pltpu.VMEM)
     return pl.pallas_call(
         attend_kernel,
-        out_shape=jax.ShapeDtypeStruct((2 * ROWS, WIDTH // 2), jnp.bfloat16),
+        out_shape=jax.ShapeDtypeStruct((GROUPS, HEAD, QROWS), jnp.bfloat16),
         in_specs=[pl.BlockSpec(memory_space=pltpu.SMEM), vmem, vmem, vmem, vmem],
         out_specs=vmem,
         scratch_shapes=[
             pltpu.VMEM((HEAD, TOKENS), jnp.bfloat16),
-            pltpu.VMEM((2 * GROUPS, QROWS, 2 * HEAD), jnp.bfloat16),
+            pltpu.VMEM((2 * GROUPS, SPAN * 8, HEAD), jnp.bfloat16),
             pltpu.VMEM((TILE, QROWS), jnp.float32),
             pltpu.VMEM((TILE, QROWS), jnp.float32),
             pltpu.VMEM((GROUPS + 1, HEAD, QROWS), jnp.float32),
@@ -610,14 +621,28 @@
     pl.semaphore_signal(barrier, inc=1, device_id={"tp": down}, device_id_type=MESH)
     lax.fori_loop(1, CP, greet, 0)
 
-    wide_row = lax.broadcasted_iota(jnp.int32, (ROWS, 2 * ROWS), 0)
-    wide_column = lax.broadcasted_iota(jnp.int32, (ROWS, 2 * ROWS), 1)
-    for h in range(2):
-        source = (wide_row // PORTION) * 8 + h * PORTION + lax.rem(wide_row, PORTION)
-        select = (wide_column == source).astype(jnp.float32).astype(jnp.bfloat16)
-        heads[:, h * (WIDTH // 2) : (h + 1) * (WIDTH // 2)] = jnp.dot(
-            select, heads_ref[...], preferred_element_type=jnp.float32
+    turned_row = lax.broadcasted_iota(jnp.int32, (QROWS, QROWS), 0)
+    turned_column = lax.broadcasted_iota(jnp.int32, (QROWS, QROWS), 1)
+    rows = SPAN * PORTION
+    head, at_row = turned_row // rows, lax.rem(turned_row, rows)
+    source = (
+        lax.rem(head, 4) * 2 * rows
+        + (at_row // PORTION) * 2 * PORTION
+        + (head // 4) * PORTION
+        + lax.rem(at_row, PORTION)
+    )
+    select = (turned_column == source).astype(jnp.float32).astype(jnp.bfloat16)
+    for g in range(GROUPS):
+        part = lax.dot_general(
+            select,
+            heads_ref[g],
+            (((1,), (1,)), ((), ())),
+            preferred_element_type=jnp.float32,
         ).astype(jnp.bfloat16)
+        for h in range(HEADS):
+            heads[g * rows : (g + 1) * rows, h * HEAD : (h + 1) * HEAD] = part[
+                h * rows : (h + 1) * rows
+            ]
 
     def product(n, c):
         columns = slice(FIRST[c] * HEAD, (FIRST[c] + CHUNKS[c]) * HEAD)
@@ -692,13 +717,13 @@
     origin = (lax.rem(row, BLOCK) // 4) * 8 + (row // BLOCK) * 4 + lax.rem(row, 4)
     to_place = (column == origin).astype(jnp.float32).astype(jnp.bfloat16)
 
-    def acopy(c, k, target, slot):
+    def acopy(c, target, slot):
         at = pl.ds(FIRST[c], CHUNKS[c])
         return pltpu.make_async_remote_copy(
             src_ref=spread.at[target, at],
             dst_ref=landed.at[slot, at],
-            send_sem=a_send.at[c, k],
-            recv_sem=a_recv.at[c, k],
+            send_sem=a_send.at[c],
+            recv_sem=a_recv.at[c],
             device_id={"cp": target},
             device_id_type=MESH,
         )
@@ -723,19 +748,14 @@
             landed[me, at] = spread[me, at]
 
         def send(k, carry):
-            acopy(c, k, lax.rem(me + k, CP), me).start()
+            acopy(c, lax.rem(me + k, CP), me).start()
             return carry
 
         lax.fori_loop(1, CP, send, 0)
 
     def place(c):
-        def wait(k, carry):
-            copy = acopy(c, k, lax.rem(me + k, CP), lax.rem(me + CP - k, CP))
-            copy.wait_send()
-            copy.wait_recv()
-            return carry
-
-        lax.fori_loop(1, CP, wait, 0)
+        everyone = landed.at[pl.ds(0, CP - 1), pl.ds(FIRST[c], CHUNKS[c])]
+        pltpu.make_async_copy(everyone, everyone, a_recv.at[c]).wait()
         rows = jnp.concatenate(
             [
                 landed[:, at].astype(jnp.float32).reshape(ROWS, HEAD).astype(jnp.bfloat16)
@@ -779,6 +799,8 @@
     for c in range(len(CHUNKS)):
         for copy in (*far_copies[c], *near_copies[c]):
             copy.wait_send()
+        everyone = spread.at[pl.ds(0, CP - 1), pl.ds(FIRST[c], CHUNKS[c])]
+        pltpu.make_async_copy(everyone, everyone, a_send.at[c]).wait()
 
 
 def output_call(slot_rows, heads, wo):
@@ -802,7 +824,7 @@
             pltpu.VMEM((CP, PIECES, 8, HEAD), bf16),
             pltpu.VMEM((PIECES, ROWS, HEAD), jnp.float32),
             dma((4,)), dma((4 * len(CHUNKS),)), dma((4 * len(CHUNKS),)),
-            dma((len(CHUNKS), CP)), dma((len(CHUNKS), CP)),
+            dma((len(CHUNKS),)), dma((len(CHUNKS),)),
         ],
         compiler_params=pltpu.CompilerParams(
             collective_id=1, has_side_effects=True, vmem_limit_bytes=40 * 1024 * 1024
@@ -823,7 +845,7 @@
         for a in (hidden, query_weight, key_matrix, value_matrix, output_weight)
     )
     keys, values, queries, marks = gather_call(
-        bounds, hidden, query_weight, key_matrix, value_matrix, inverse
+        pltpu.with_memory_space_constraint(bounds, pltpu.HBM), hidden, query_weight, key_matrix, value_matrix, inverse
     )
     heads = attend_call(
         bounds,

time: 96.4 us -> 89 us (0.923); the launches traced: 96.7 us -> 88 us
  Pallas kernels: 94.7 us -> 86.7 us
    pallas_call x1, Pallas kernels: 50.4 us -> 47 us  [gather_call(): pl.pallas_call(gather_kernel, out_shape=(kv, kv, jax.ShapeDtypeStruct((CP...]
    pallas_call x1, Pallas kernels: 31.1 us -> 28.5 us  [output_call(): pl.pallas_call(output_kernel, out_shape=jax.ShapeDtypeStruct((ROWS, WIDTH...]
    pallas_call x1, Pallas kernels: 13.2 us -> 11.2 us  [attend_call(): pl.pallas_call(attend_kernel, out_shape=jax.ShapeDtypeStruct((GROUPS, HEA...]
where the time goes in v4:
time: 89 us; the launch traced here: 88 us
  Pallas kernels  86.7 us (97%)
  local copies, waits for them, and re-layouts  0.92 us (1%)
    pallas_call x1, Pallas kernels, gather_call(): pl.pallas_call(gather_kernel, out_shape=(kv, kv, jax.ShapeDtypeStruct((CP...  47 us
    pallas_call x1, Pallas kernels, output_call(): pl.pallas_call(output_kernel, out_shape=jax.ShapeDtypeStruct((ROWS, WIDTH...  28.5 us
    pallas_call x1, Pallas kernels, attend_call(): pl.pallas_call(attend_kernel, out_shape=jax.ShapeDtypeStruct((GROUPS, HEA...  11.2 us

profile of v4, /device:TPU:1, one launch (start us, length us, event | category | flops | bytes accessed | tf_op | source)
XLA Modules:
  0.0 88.0 jit_solution(9927440660573670243)
XLA Ops:
  0.0 0.1 maximum_bitcast_fusion.inverse_ref
  0.1 0.0 copy-start
  0.1 47.0 %gather_project.1 = (bf16[4,4,2,256,128]{4,3,2,1,0:T(8,128)(2,1)S(1)}, bf16[4,4,2,256,128]{4,3,2,1,0:T(8,128)(2,1)S(1)}, bf16[32,2,8,512]{3,2,1,0:T(8,128)(2,1)S(1)}, bf16[8192,128]{1,0:T(8,128)(2,1)S(1)}) custom-call(s32[9]{0:T(128)} %bounds_ref.1, bf16[256,1024]{1,0:T(8,128)(2,1)} %hidden_ref.1, bf16[4096,1024]{1,0:T(8,128)(2,1)} %wq_ref.1, ...), custom_call_target="tpu_custom_call" | custom-call | tf_op jit(solution)/shard_map/gather_project/pallas_call | solution.py:404
  47.1 0.0 copy-done
  47.1 0.0 copy-start.1
  47.2 11.2 %attend.1.heads_ref = bf16[8,128,256]{2,1,0:T(8,128)(2,1)S(1)} custom-call(s32[9]{0:T(128)S(1)} %copy-done, bf16[512,512]{1,0:T(8,128)(2,1)S(1)} %bitcast.7, bf16[8192,128]{1,0:T(8,128)(2,1)S(1)} %bitcast.5, bf16[8192,128]{1,0:T(8,128)(2,1)S(1)} %bitcast.6, bf16[8192,128]{1,0:T(8,128)(2,1)S(1)} %get-tuple-element.12.mark_ref), custom_call_target="tpu_custom_call" | custom-call | tf_op jit(solution)/shard_map/attend/pallas_call | solution.py:574
  58.3 0.0 copy-done.1
  58.3 0.2 convert_reduce_fusion
  58.5 0.1 iota_add_fusion
  58.6 0.1 add.36.slot_ref
  58.7 28.5 %project_out.1 = bf16[256,1024]{1,0:T(8,128)(2,1)S(1)} custom-call(s32[1,256]{1,0:T(1,128)S(1)} %add.36.slot_ref, bf16[8,128,256]{2,1,0:T(8,128)(2,1)S(1)} %attend.1.heads_ref, bf16[1024,4096]{1,0:T(8,128)(2,1)} %wo_ref.1), custom_call_target="tpu_custom_call" | custom-call | tf_op jit(solution)/shard_map/project_out/pallas_call | solution.py:811
  87.2 0.8 copy.9
  (2 shorter events, 0.0 us)
Async XLA Ops:
  0.1 47.0 %copy-start = (s32[9]{0:T(128)S(1)}, s32[9]{0:T(128)}, u32[]{:S(2)}) copy-start(s32[9]{0:T(128)} %bounds_ref.1) | copy-start | bytes 112
  47.1 11.2 %copy-start.1 = (s32[64]{0:T(128)S(1)}, s32[64]{0:T(128)}, u32[]{:S(2)}) copy-start(s32[64]{0:T(128)} %param.13) | copy-start | bytes 772

commit v5 on v4

--- a/solution.py
+++ b/solution.py
@@ -108,7 +108,7 @@
         return pltpu.make_async_remote_copy(
             src_ref=ref,
             dst_ref=ref,
-            send_sem=z_send.at[n],
+            send_sem=z_send.at[0],
             recv_sem=z_recv.at[n],
             device_id={"tp": target},
             device_id_type=MESH,
@@ -116,18 +116,26 @@
 
     own = [
         (
-            zcopy(4 * r, up, tp, STARTS[r], SIZES[r]),
-            zcopy(4 * r + 1, down, tp, STARTS[r], SIZES[r]),
+            zcopy(2 * r, up, tp, STARTS[r], SIZES[r]),
+            zcopy(2 * r, down, tp, STARTS[r], SIZES[r]),
         )
         for r in range(PARTS)
     ]
     fwd = [
         (
-            zcopy(4 * r + 2, down, up, STARTS[r], SIZES[r] // 2),
-            zcopy(4 * r + 3, up, down, STARTS[r] + SIZES[r] // 2, SIZES[r] // 2),
+            zcopy(2 * r + 1, down, up, STARTS[r], SIZES[r] // 2),
+            zcopy(2 * r + 1, up, down, STARTS[r] + SIZES[r] // 2, SIZES[r] // 2),
         )
         for r in range(PARTS)
     ]
+
+    def wait_for(ref, semaphore):
+        pltpu.make_async_copy(ref, ref, semaphore).wait()
+
+    def arrived_z(n, r, owners):
+        wait_for(
+            full.at[pl.ds(STARTS[r], SIZES[r]), pl.ds(0, owners * WIDTH)], z_recv.at[2 * r + n]
+        )
     for copy in (*own[0], *own[1]):
         copy.start()
     for target in along_x:
@@ -135,8 +143,7 @@
     bring_bounds.wait()
 
     def relay_z(r):
-        for copy in own[r]:
-            copy.wait_recv()
+        arrived_z(0, r, 2)
         for copy in fwd[r]:
             copy.start()
         if r + 2 < PARTS:
@@ -191,7 +198,6 @@
     def gather(which, r):
         buffer = (k_ref, v_ref)[which]
         a, b = ((xcoord, ycoord), (ycoord, xcoord))[which]
-        base = (which * PARTS + r) * 12
 
         def neighbour(along, step):
             if along == 0:
@@ -205,8 +211,8 @@
             return pltpu.make_async_remote_copy(
                 src_ref=ref,
                 dst_ref=ref,
-                send_sem=g_send.at[base + n],
-                recv_sem=g_recv.at[base + n],
+                send_sem=g_send.at[r],
+                recv_sem=g_recv.at[r, n],
                 device_id={"cp": target},
                 device_id_type=MESH,
             )
@@ -230,29 +236,29 @@
         return dict(
             ring1=(
                 copy(0, piece(a, 0, size), neighbour(0, 1)),
-                copy(1, piece(a, 0, size), neighbour(0, 3)),
+                copy(0, piece(a, 0, size), neighbour(0, 3)),
             ),
-            ring1_far=(copy(2, piece(a, 0, size), neighbour(0, 2)),)
+            ring1_far=(copy(1, piece(a, 0, size), neighbour(0, 2)),)
             if STRAIGHT1[r]
             else (
-                copy(2, piece(a_prev, 0, half), neighbour(0, 1)),
-                copy(3, piece(a_next, half, half), neighbour(0, 3)),
+                copy(1, piece(a_prev, 0, half), neighbour(0, 1)),
+                copy(1, piece(a_next, half, half), neighbour(0, 3)),
             ),
             ring2=(
-                copy(4, line(b, 0, 4), neighbour(1, 1)),
-                copy(5, line(b, 0, 4), neighbour(1, 3)),
+                copy(2, line(b, 0, 4), neighbour(1, 1)),
+                copy(2, line(b, 0, 4), neighbour(1, 3)),
             ),
-            ring2_far=(copy(6, line(b, 0, 4), neighbour(1, 2)),)
+            ring2_far=(copy(3, line(b, 0, 4), neighbour(1, 2)),)
             if STRAIGHT2[r]
             else (
-                copy(6, line(b_prev, 0, 2), neighbour(1, 1)),
-                copy(7, line(b_next, 2, 2), neighbour(1, 3)),
+                copy(3, line(b_prev, 0, 2), neighbour(1, 1)),
+                copy(3, line(b_next, 2, 2), neighbour(1, 3)),
             ),
             across=(
-                copy(8, line(b, 0, 4), partner),
-                copy(9, line(b_prev, 0, 4), partner),
-                copy(10, line(b_next, 0, 4), partner),
-                copy(11, line(b_far, 0, 4), partner),
+                copy(4, line(b, 0, 4), partner),
+                copy(4, line(b_prev, 0, 4), partner),
+                copy(4, line(b_next, 0, 4), partner),
+                copy(4, line(b_far, 0, 4), partner),
             ),
         )
 
@@ -264,9 +270,15 @@
                 copy.start()
 
     def arrived(r, name):
-        for flow in flows[r]:
-            for copy in flow[name]:
-                copy.wait_recv()
+        rows = pl.ds(STARTS[r], SIZES[r])
+        n, ref = {
+            "ring1": (0, k_ref.at[0, :, core, rows]),
+            "ring1_far": (1, k_ref.at[0, pl.ds(0, 2), core, rows]),
+            "ring2": (2, k_ref.at[:, :, core, rows]),
+            "ring2_far": (3, k_ref.at[pl.ds(0, 2), :, core, rows]),
+            "across": (4, k_ref.at[:, :, :, rows]),
+        }[name]
+        wait_for(ref, g_recv.at[r, n])
 
     def across(r, which):
         for flow in flows[r]:
@@ -274,8 +286,7 @@
                 flow["across"][n].start()
 
     def s0(r):
-        for copy in fwd[r]:
-            copy.wait_recv()
+        arrived_z(1, r, 1)
         rows = pl.ds(STARTS[r], SIZES[r])
         raw = jnp.dot(full[rows, :], wkv[...], preferred_element_type=jnp.float32)
         k_ref[xcoord, ycoord, core, rows] = rotate(raw[:, :HEAD], STARTS[r], SIZES[r]).astype(
@@ -387,13 +398,8 @@
     spread_done(1)
     for r in range(PARTS):
         arrived(r, "across")
-        for flow in flows[r]:
-            for name in ("ring1", "ring1_far", "ring2", "ring2_far", "across"):
-                for copy in flow[name]:
-                    copy.wait_send()
-    for group in (*own, *fwd):
-        for copy in group:
-            copy.wait_send()
+        wait_for(mark_ref.at[pl.ds(0, 62 * SIZES[r])], g_send.at[r])
+    wait_for(full.at[:, pl.ds(0, 3 * WIDTH)], z_send.at[0])
 
 
 def gather_call(bounds, hidden, wq, wk, wv, inverse):
@@ -419,8 +425,8 @@
             pltpu.VMEM((2, CP, 8, WIDTH // 2), jnp.bfloat16),
             pltpu.VMEM((ROWS, HEAD), jnp.float32),
             pltpu.VMEM((ROWS, HEAD), jnp.float32),
-            dma((5,)), dma((4 * PARTS,)), dma((4 * PARTS,)),
-            dma((24 * PARTS,)), dma((24 * PARTS,)), dma((2,)), dma((2,)),
+            dma((5,)), dma((1,)), dma((2 * PARTS,)),
+            dma((PARTS,)), dma((PARTS, 5)), dma((2,)), dma((2,)),
             pltpu.SMEM((9,), jnp.int32), pltpu.SemaphoreType.REGULAR((2,)),
         ],
         compiler_params=pltpu.CompilerParams(
@@ -652,7 +658,7 @@
         return pltpu.make_async_remote_copy(
             src_ref=src,
             dst_ref=dst,
-            send_sem=z_send.at[n],
+            send_sem=z_send.at[0],
             recv_sem=z_recv.at[n],
             device_id={"tp": target},
             device_id_type=MESH,
@@ -665,14 +671,14 @@
         at = pl.ds(FIRST[c], count)
         far_copies.append(
             (
-                remote(4 * c, far.at[0, at], far_in.at[0, at], up),
-                remote(4 * c + 1, far.at[1, at], far_in.at[1, at], down),
+                remote(3 * c, far.at[0, at], far_in.at[0, at], up),
+                remote(3 * c + 1, far.at[1, at], far_in.at[1, at], down),
             )
         )
         near_copies.append(
             (
-                remote(4 * c + 2, near.at[0, at], near_in.at[0, at], up),
-                remote(4 * c + 3, near.at[1, at], near_in.at[1, at], down),
+                remote(3 * c + 2, near.at[0, at], near_in.at[0, at], up),
+                remote(3 * c + 2, near.at[1, at], near_in.at[1, at], down),
             )
         )
 
@@ -729,8 +735,8 @@
         )
 
     def finish_sum(c):
-        for copy in near_copies[c]:
-            copy.wait_recv()
+        both = near_in.at[:, pl.ds(FIRST[c], CHUNKS[c])]
+        pltpu.make_async_copy(both, both, z_recv.at[3 * c + 2]).wait()
         total = jnp.concatenate(
             [
                 (
@@ -797,10 +803,10 @@
     for c in range(len(CHUNKS)):
         place(c)
     for c in range(len(CHUNKS)):
-        for copy in (*far_copies[c], *near_copies[c]):
-            copy.wait_send()
         everyone = spread.at[pl.ds(0, CP - 1), pl.ds(FIRST[c], CHUNKS[c])]
         pltpu.make_async_copy(everyone, everyone, a_send.at[c]).wait()
+    sent = wo.at[0, pl.ds(0, 3 * ROWS)]
+    pltpu.make_async_copy(sent, sent, z_send.at[0]).wait()
 
 
 def output_call(slot_rows, heads, wo):
@@ -823,7 +829,7 @@
             pltpu.VMEM((CP, PIECES, 8, HEAD), bf16),
             pltpu.VMEM((CP, PIECES, 8, HEAD), bf16),
             pltpu.VMEM((PIECES, ROWS, HEAD), jnp.float32),
-            dma((4,)), dma((4 * len(CHUNKS),)), dma((4 * len(CHUNKS),)),
+            dma((4,)), dma((1,)), dma((3 * len(CHUNKS),)),
             dma((len(CHUNKS),)), dma((len(CHUNKS),)),
         ],
         compiler_params=pltpu.CompilerParams(

time: 89 us -> 85.2 us (0.957); the launches traced: 88 us -> 85.5 us
  Pallas kernels: 86.7 us -> 84.2 us
    pallas_call x1, Pallas kernels: 47 us -> 44.8 us  [gather_call(): pl.pallas_call(gather_kernel, out_shape=(kv, kv, jax.ShapeDtypeStruct((CP...]
where the time goes in v5:
time: 85.2 us; the launch traced here: 85.5 us
  Pallas kernels  84.2 us (99%)
  local copies, waits for them, and re-layouts  0.92 us (1%)
    pallas_call x1, Pallas kernels, gather_call(): pl.pallas_call(gather_kernel, out_shape=(kv, kv, jax.ShapeDtypeStruct((CP...  44.8 us
    pallas_call x1, Pallas kernels, output_call(): pl.pallas_call(output_kernel, out_shape=jax.ShapeDtypeStruct((ROWS, WIDTH...  28.2 us
    pallas_call x1, Pallas kernels, attend_call(): pl.pallas_call(attend_kernel, out_shape=jax.ShapeDtypeStruct((GROUPS, HEA...  11.2 us

profile of v5, /device:TPU:1, one launch (start us, length us, event | category | flops | bytes accessed | tf_op | source)
XLA Modules:
  0.0 85.5 jit_solution(11390711638815925721)
XLA Ops:
  0.0 0.1 maximum_bitcast_fusion.inverse_ref
  0.1 0.0 copy-start
  0.1 44.8 %gather_project.1 = (bf16[4,4,2,256,128]{4,3,2,1,0:T(8,128)(2,1)S(1)}, bf16[4,4,2,256,128]{4,3,2,1,0:T(8,128)(2,1)S(1)}, bf16[32,2,8,512]{3,2,1,0:T(8,128)(2,1)S(1)}, bf16[8192,128]{1,0:T(8,128)(2,1)S(1)}) custom-call(s32[9]{0:T(128)} %bounds_ref.1, bf16[256,1024]{1,0:T(8,128)(2,1)} %hidden_ref.1, bf16[4096,1024]{1,0:T(8,128)(2,1)} %wq_ref.1, ...), custom_call_target="tpu_custom_call" | custom-call | tf_op jit(solution)/shard_map/gather_project/pallas_call | solution.py:410
  44.9 0.0 copy-done
  44.9 0.0 copy-start.1
  44.9 11.2 %attend.1.heads_ref = bf16[8,128,256]{2,1,0:T(8,128)(2,1)S(1)} custom-call(s32[9]{0:T(128)S(1)} %copy-done, bf16[512,512]{1,0:T(8,128)(2,1)S(1)} %bitcast.7, bf16[8192,128]{1,0:T(8,128)(2,1)S(1)} %bitcast.5, bf16[8192,128]{1,0:T(8,128)(2,1)S(1)} %bitcast.6, bf16[8192,128]{1,0:T(8,128)(2,1)S(1)} %get-tuple-element.12.mark_ref), custom_call_target="tpu_custom_call" | custom-call | tf_op jit(solution)/shard_map/attend/pallas_call | solution.py:580
  56.1 0.0 copy-done.1
  56.1 0.2 convert_reduce_fusion
  56.3 0.1 iota_add_fusion
  56.4 0.1 add.36.slot_ref
  56.5 28.2 %project_out.1 = bf16[256,1024]{1,0:T(8,128)(2,1)S(1)} custom-call(s32[1,256]{1,0:T(1,128)S(1)} %add.36.slot_ref, bf16[8,128,256]{2,1,0:T(8,128)(2,1)S(1)} %attend.1.heads_ref, bf16[1024,4096]{1,0:T(8,128)(2,1)} %wo_ref.1), custom_call_target="tpu_custom_call" | custom-call | tf_op jit(solution)/shard_map/project_out/pallas_call | solution.py:817
  84.7 0.8 copy.9
  (2 shorter events, 0.0 us)
Async XLA Ops:
  0.1 44.8 %copy-start = (s32[9]{0:T(128)S(1)}, s32[9]{0:T(128)}, u32[]{:S(2)}) copy-start(s32[9]{0:T(128)} %bounds_ref.1) | copy-start | bytes 112
  44.9 11.2 %copy-start.1 = (s32[64]{0:T(128)S(1)}, s32[64]{0:T(128)}, u32[]{:S(2)}) copy-start(s32[64]{0:T(128)} %param.13) | copy-start | bytes 772

commit v6 on v5

--- a/solution.py
+++ b/solution.py
@@ -446,7 +446,7 @@
 
 def attend_kernel(
     bounds_ref, q_ref, k_ref, v_ref, mark_ref, o_ref,
-    turned, penalty_ref, even, odd, mixed_ref, total_ref,
+    turned, penalty_ref, even, odd, even_soft, odd_soft, mixed_ref, total_ref,
 ):
     rows = SPAN * 8
     factor = math.log2(math.e) / math.sqrt(HEAD)
@@ -518,43 +518,50 @@
             largest = top if part == 0 else jnp.maximum(largest, top)
         return largest
 
-    def soften(item, ref, largest, state):
+    def soften(item, ref, soft, largest, top, total):
         g, j = item
-        top, total, mixed = state
         top = jnp.where(g == j, 0.5 * PENALTY, top)
-        start = jnp.minimum(j, GROUPS - 1) * TILE
         new_top = jnp.maximum(top, largest)
         shrink = jnp.exp2((top - new_top) * factor)
-        total, mixed = total * shrink, mixed * shrink
+        total = total * shrink
         for first in range(0, TILE, PIECE):
             piece = slice(first, first + PIECE)
             weights = jnp.exp2((ref[piece, :] - new_top) * factor)
             total = total + jnp.sum(weights, axis=0, keepdims=True)
-            keys = pl.ds(pl.multiple_of(start + first, PIECE), PIECE)
-            mixed = mixed + jnp.dot(
-                turned[:, keys], weights.astype(jnp.bfloat16), preferred_element_type=jnp.float32
-            )
+            soft[piece, :] = weights.astype(jnp.bfloat16)
+        total_ref[g] = total
+        return new_top, total, shrink
+
+    def blend(item, soft, shrink, mixed):
+        g, j = item
+        first = pl.multiple_of(jnp.minimum(j, GROUPS - 1) * TILE, TILE)
+        mixed = mixed * shrink + jnp.dot(
+            turned[:, pl.ds(first, TILE)], soft[...], preferred_element_type=jnp.float32
+        )
         mixed_ref[g] = mixed
-        total_ref[g] = total
-        return new_top, total, mixed
+        return mixed
 
     count = lax.fori_loop(0, GROUPS, lambda g, n: n + g + 1 - lowest(g), jnp.int32(0))
     zero = jnp.int32(0)
     highest = score((zero, zero), even)
+    odd_soft[...] = jnp.zeros_like(odd_soft)
 
     def pair(n, carry):
-        g, j, largest, *state = carry
+        g, j, largest, last_g, last_j, last_shrink, top, total, mixed = carry
         item = (g, j)
         second = following(item)
         second_largest = score(second, odd)
-        state = soften(item, even, largest, state)
+        mixed = blend((last_g, last_j), odd_soft, last_shrink, mixed)
+        top, total, shrink = soften(item, even, even_soft, largest, top, total)
         third = following(second)
         third = (jnp.minimum(third[0], GROUPS), jnp.minimum(third[1], GROUPS))
         largest = score(third, even)
-        state = soften(second, odd, second_largest, state)
-        return (*third, largest, *state)
-
-    lax.fori_loop(
+        mixed = blend(item, even_soft, shrink, mixed)
+        top, total, shrink = soften(second, odd, odd_soft, second_largest, top, total)
+        return (*third, largest, *second, shrink, top, total, mixed)
+
+    row_of = functools.partial(jnp.full, (1, QROWS), dtype=jnp.float32)
+    carry = lax.fori_loop(
         0,
         (count + 1) // 2,
         pair,
@@ -562,11 +569,15 @@
             zero,
             zero,
             highest,
-            jnp.full((1, QROWS), 0.5 * PENALTY, jnp.float32),
-            jnp.zeros((1, QROWS), jnp.float32),
+            jnp.int32(GROUPS),
+            zero,
+            row_of(0.0),
+            row_of(0.5 * PENALTY),
+            row_of(0.0),
             jnp.zeros((HEAD, QROWS), jnp.float32),
         ),
     )
+    blend(carry[3:5], odd_soft, carry[5], carry[8])
 
     def finish(g, carry):
         o_ref[g] = (mixed_ref[g] / total_ref[g]).astype(jnp.bfloat16)
@@ -587,6 +598,8 @@
             pltpu.VMEM((2 * GROUPS, SPAN * 8, HEAD), jnp.bfloat16),
             pltpu.VMEM((TILE, QROWS), jnp.float32),
             pltpu.VMEM((TILE, QROWS), jnp.float32),
+            pltpu.VMEM((TILE, QROWS), jnp.bfloat16),
+            pltpu.VMEM((TILE, QROWS), jnp.bfloat16),
             pltpu.VMEM((GROUPS + 1, HEAD, QROWS), jnp.float32),
             pltpu.VMEM((GROUPS + 1, 1, QROWS), jnp.float32),
         ],

time: 85.2 us -> 86 us (level)
  no operation moved by 1% of the time
where the time goes in v6:
time: 86 us; the launch traced here: 86.4 us
  Pallas kernels  85 us (99%)
  local copies, waits for them, and re-layouts  0.92 us (1%)
    pallas_call x1, Pallas kernels, gather_call(): pl.pallas_call(gather_kernel, out_shape=(kv, kv, jax.ShapeDtypeStruct((CP...  44.8 us
    pallas_call x1, Pallas kernels, output_call(): pl.pallas_call(output_kernel, out_shape=jax.ShapeDtypeStruct((ROWS, WIDTH...  28.2 us
    pallas_call x1, Pallas kernels, attend_call(): pl.pallas_call(attend_kernel, out_shape=jax.ShapeDtypeStruct((GROUPS, HEA...  12 us

profile of v6, /device:TPU:1, one launch (start us, length us, event | category | flops | bytes accessed | tf_op | source)
XLA Modules:
  0.0 86.4 jit_solution(14829670450546675675)
XLA Ops:
  0.0 0.1 maximum_bitcast_fusion.inverse_ref
  0.1 0.0 copy-start
  0.1 44.8 %gather_project.1 = (bf16[4,4,2,256,128]{4,3,2,1,0:T(8,128)(2,1)S(1)}, bf16[4,4,2,256,128]{4,3,2,1,0:T(8,128)(2,1)S(1)}, bf16[32,2,8,512]{3,2,1,0:T(8,128)(2,1)S(1)}, bf16[8192,128]{1,0:T(8,128)(2,1)S(1)}) custom-call(s32[9]{0:T(128)} %bounds_ref.1, bf16[256,1024]{1,0:T(8,128)(2,1)} %hidden_ref.1, bf16[4096,1024]{1,0:T(8,128)(2,1)} %wq_ref.1, ...), custom_call_target="tpu_custom_call" | custom-call | tf_op jit(solution)/shard_map/gather_project/pallas_call | solution.py:410
  44.9 0.0 copy-done
  44.9 0.0 copy-start.1
  44.9 12.0 %attend.1.heads_ref = bf16[8,128,256]{2,1,0:T(8,128)(2,1)S(1)} custom-call(s32[9]{0:T(128)S(1)} %copy-done, bf16[512,512]{1,0:T(8,128)(2,1)S(1)} %bitcast.7, bf16[8192,128]{1,0:T(8,128)(2,1)S(1)} %bitcast.5, bf16[8192,128]{1,0:T(8,128)(2,1)S(1)} %bitcast.6, bf16[8192,128]{1,0:T(8,128)(2,1)S(1)} %get-tuple-element.12.mark_ref), custom_call_target="tpu_custom_call" | custom-call | tf_op jit(solution)/shard_map/attend/pallas_call | solution.py:591
  56.9 0.0 copy-done.1
  57.0 0.2 convert_reduce_fusion
  57.1 0.1 iota_add_fusion
  57.2 0.1 add.36.slot_ref
  57.3 28.2 %project_out.1 = bf16[256,1024]{1,0:T(8,128)(2,1)S(1)} custom-call(s32[1,256]{1,0:T(1,128)S(1)} %add.36.slot_ref, bf16[8,128,256]{2,1,0:T(8,128)(2,1)S(1)} %attend.1.heads_ref, bf16[1024,4096]{1,0:T(8,128)(2,1)} %wo_ref.1), custom_call_target="tpu_custom_call" | custom-call | tf_op jit(solution)/shard_map/project_out/pallas_call | solution.py:830
  85.6 0.8 copy.9
  (2 shorter events, 0.0 us)
Async XLA Ops:
  0.1 44.8 %copy-start = (s32[9]{0:T(128)S(1)}, s32[9]{0:T(128)}, u32[]{:S(2)}) copy-start(s32[9]{0:T(128)} %bounds_ref.1) | copy-start | bytes 112
  44.9 12.0 %copy-start.1 = (s32[64]{0:T(128)S(1)}, s32[64]{0:T(128)}, u32[]{:S(2)}) copy-start(s32[64]{0:T(128)} %param.13) | copy-start | bytes 772

commit v7 on v5

--- a/solution.py
+++ b/solution.py
@@ -50,6 +50,22 @@
         bound = bounds_ref[i]
         start = jnp.where(tokens >= bound, bound, start)
     return start
+
+
+def to_others(me, send):
+    core, ycoord, xcoord = lax.rem(me, 2), lax.rem(me // 2, 4), me // 8
+
+    def offset(n):
+        return 2 - n + 3 * (n // 2) - 2 * (n // 3)
+
+    def step(n, carry):
+        chip = lax.rem(xcoord + offset(n // 4), 4) * 4 + lax.rem(ycoord + offset(lax.rem(n, 4)), 4)
+        send(chip * 2 + core)
+        send(chip * 2 + 1 - core)
+        return carry
+
+    lax.fori_loop(0, 15, step, 0)
+    send(me + 1 - 2 * core)
 
 
 SIZES = (64, 64, 64, 32, 32)
@@ -339,11 +355,7 @@
         qsend[r] = ordered.reshape(CP, 8, WIDTH // 2).astype(jnp.bfloat16)
         q_ref[me, r] = qsend[r, me]
 
-        def send(k, carry):
-            qcopy(r, lax.rem(me + k, CP), me).start()
-            return carry
-
-        lax.fori_loop(1, CP, send, 0)
+        to_others(me, lambda target: qcopy(r, target, me).start())
 
     def spread_done(r):
         sent, landed = qsend.at[r, pl.ds(0, CP - 1)], q_ref.at[pl.ds(0, CP - 1), r]
@@ -753,11 +765,7 @@
             spread[:, at] = picked[:, columns].reshape(CP, 8, HEAD).astype(jnp.bfloat16)
             landed[me, at] = spread[me, at]
 
-        def send(k, carry):
-            acopy(c, lax.rem(me + k, CP), me).start()
-            return carry
-
-        lax.fori_loop(1, CP, send, 0)
+        to_others(me, lambda target: acopy(c, target, me).start())
 
     def place(c):
         everyone = landed.at[pl.ds(0, CP - 1), pl.ds(FIRST[c], CHUNKS[c])]

time: 85.2 us -> 87.5 us (1.027)
  Pallas kernels: 84.2 us -> 86.1 us
    pallas_call x1, Pallas kernels: 11.2 us -> 12.9 us  [attend_call(): pl.pallas_call(attend_kernel, out_shape=jax.ShapeDtypeStruct((GROUPS, HEA...]
where the time goes in v7:
time: 87.5 us; the launch traced here: 87.4 us
  Pallas kernels  86.1 us (98%)
  local copies, waits for them, and re-layouts  0.92 us (1%)
    pallas_call x1, Pallas kernels, gather_call(): pl.pallas_call(gather_kernel, out_shape=(kv, kv, jax.ShapeDtypeStruct((CP...  45.3 us
    pallas_call x1, Pallas kernels, output_call(): pl.pallas_call(output_kernel, out_shape=jax.ShapeDtypeStruct((ROWS, WIDTH...  27.8 us
    pallas_call x1, Pallas kernels, attend_call(): pl.pallas_call(attend_kernel, out_shape=jax.ShapeDtypeStruct((GROUPS, HEA...  12.9 us

profile of v7, /device:TPU:1, one launch (start us, length us, event | category | flops | bytes accessed | tf_op | source)
XLA Modules:
  0.0 87.4 jit_solution(12700452855478991640)
XLA Ops:
  0.0 0.1 maximum_bitcast_fusion.inverse_ref
  0.1 0.0 copy-start
  0.1 45.3 %gather_project.1 = (bf16[4,4,2,256,128]{4,3,2,1,0:T(8,128)(2,1)S(1)}, bf16[4,4,2,256,128]{4,3,2,1,0:T(8,128)(2,1)S(1)}, bf16[32,2,8,512]{3,2,1,0:T(8,128)(2,1)S(1)}, bf16[8192,128]{1,0:T(8,128)(2,1)S(1)}) custom-call(s32[9]{0:T(128)} %bounds_ref.1, bf16[256,1024]{1,0:T(8,128)(2,1)} %hidden_ref.1, bf16[4096,1024]{1,0:T(8,128)(2,1)} %wq_ref.1, ...), custom_call_target="tpu_custom_call" | custom-call | tf_op jit(solution)/shard_map/gather_project/pallas_call | solution.py:422
  45.4 0.0 copy-done
  45.5 0.0 copy-start.1
  45.5 12.9 %attend.1.heads_ref = bf16[8,128,256]{2,1,0:T(8,128)(2,1)S(1)} custom-call(s32[9]{0:T(128)S(1)} %copy-done, bf16[512,512]{1,0:T(8,128)(2,1)S(1)} %bitcast.7, bf16[8192,128]{1,0:T(8,128)(2,1)S(1)} %bitcast.5, bf16[8192,128]{1,0:T(8,128)(2,1)S(1)} %bitcast.6, bf16[8192,128]{1,0:T(8,128)(2,1)S(1)} %get-tuple-element.12.mark_ref), custom_call_target="tpu_custom_call" | custom-call | tf_op jit(solution)/shard_map/attend/pallas_call | solution.py:592
  58.4 0.0 copy-done.1
  58.4 0.2 convert_reduce_fusion
  58.6 0.1 iota_add_fusion
  58.7 0.1 add.36.slot_ref
  58.8 27.8 %project_out.1 = bf16[256,1024]{1,0:T(8,128)(2,1)S(1)} custom-call(s32[1,256]{1,0:T(1,128)S(1)} %add.36.slot_ref, bf16[8,128,256]{2,1,0:T(8,128)(2,1)S(1)} %attend.1.heads_ref, bf16[1024,4096]{1,0:T(8,128)(2,1)} %wo_ref.1), custom_call_target="tpu_custom_call" | custom-call | tf_op jit(solution)/shard_map/project_out/pallas_call | solution.py:825
  86.6 0.8 copy.9
  (2 shorter events, 0.0 us)
Async XLA Ops:
  0.1 45.4 %copy-start = (s32[9]{0:T(128)S(1)}, s32[9]{0:T(128)}, u32[]{:S(2)}) copy-start(s32[9]{0:T(128)} %bounds_ref.1) | copy-start | bytes 112
  45.5 12.9 %copy-start.1 = (s32[64]{0:T(128)S(1)}, s32[64]{0:T(128)}, u32[]{:S(2)}) copy-start(s32[64]{0:T(128)} %param.13) | copy-start | bytes 772

commit v8 on v5

--- a/solution.py
+++ b/solution.py
@@ -36,14 +36,6 @@
     return jnp.where(wavelength < rope_context / 4.0, inverse, longer)
 
 
-def slots_of(block_owner):
-    blocks = jnp.arange(NBLK, dtype=jnp.int32)
-    same = block_owner[:, None] == block_owner[None, :]
-    earlier = blocks[None, :] < blocks[:, None]
-    rank = jnp.sum((same & earlier).astype(jnp.int32), axis=1)
-    return block_owner * 2 + rank
-
-
 def starts_of(tokens, bounds_ref):
     start = jnp.zeros_like(tokens)
     for i in range(1, 8):
@@ -62,10 +54,10 @@
 
 
 def gather_kernel(
-    bounds_hbm, hidden_ref, wq_ref, wk_ref, wv_ref, inverse_ref,
-    k_ref, v_ref, q_ref, mark_ref,
+    bounds_hbm, owner_hbm, hidden_ref, wq_ref, wk_ref, wv_ref, inverse_ref,
+    k_ref, v_ref, q_ref, mark_ref, slot_ref,
     full, wq, wkv, qtmp, qsend, cosine, sine,
-    w_sem, z_send, z_recv, g_send, g_recv, q_send, q_recv, bounds_ref, met,
+    w_sem, z_send, z_recv, g_send, g_recv, q_send, q_recv, bounds_ref, owner_ref, met,
 ):
     me = lax.axis_index("cp")
     tp = lax.axis_index("tp")
@@ -83,8 +75,10 @@
         pltpu.make_async_copy(wq_ref, wq, w_sem.at[2]),
     ]
     bring_bounds = pltpu.make_async_copy(bounds_hbm, bounds_ref, w_sem.at[4])
+    bring_owner = pltpu.make_async_copy(owner_hbm, owner_ref, w_sem.at[5])
     bring.start()
     bring_bounds.start()
+    bring_owner.start()
     for copy in weights:
         copy.start()
 
@@ -178,6 +172,18 @@
     weights[0].wait()
     weights[1].wait()
     weights[2].wait()
+
+    def slots():
+        spot = lax.broadcasted_iota(jnp.int32, (8, ROWS), 1)
+        block = spot // PORTION
+        owner = jnp.zeros_like(spot)
+        for b in range(NBLK):
+            owner = jnp.where(block == b, owner_ref[b], owner)
+        rank = jnp.zeros_like(spot)
+        for b in range(NBLK - 1):
+            rank = rank + ((block > b) & (owner == owner_ref[b])).astype(jnp.int32)
+        place = (owner * 2 + rank) * PORTION + lax.rem(spot, PORTION)
+        slot_ref[...] = place
 
     def rotate(raw, row, count):
         table = pl.ds(row, count)
@@ -353,6 +359,8 @@
     relay_z(0)
     pl.semaphore_wait(met.at[0], 3)
     signal(met.at[1], partner)
+    bring_owner.wait()
+    slots()
     lax.fori_loop(NBLK // 2, NBLK, mark, 0)
     relay_z(1)
     pl.semaphore_wait(met.at[1], 1)
@@ -402,7 +410,7 @@
     wait_for(full.at[:, pl.ds(0, 3 * WIDTH)], z_send.at[0])
 
 
-def gather_call(bounds, hidden, wq, wk, wv, inverse):
+def gather_call(bounds, owner, hidden, wq, wk, wv, inverse):
     vmem = pl.BlockSpec(memory_space=pltpu.VMEM)
     hbm = pl.BlockSpec(memory_space=pltpu.HBM)
     kv = jax.ShapeDtypeStruct((4, 4, 2, ROWS, HEAD), jnp.bfloat16)
@@ -414,9 +422,10 @@
             kv,
             jax.ShapeDtypeStruct((CP, 2, 8, WIDTH // 2), jnp.bfloat16),
             jax.ShapeDtypeStruct((TOKENS, HEAD), jnp.bfloat16),
+            jax.ShapeDtypeStruct((8, ROWS), jnp.int32),
         ),
-        in_specs=[hbm, hbm, hbm, hbm, hbm, vmem],
-        out_specs=(vmem, vmem, vmem, vmem),
+        in_specs=[hbm, hbm, hbm, hbm, hbm, hbm, vmem],
+        out_specs=(vmem, vmem, vmem, vmem, vmem),
         scratch_shapes=[
             pltpu.VMEM((ROWS, TP * WIDTH), jnp.bfloat16),
             pltpu.VMEM((TP * WIDTH, WIDTH), jnp.bfloat16),
@@ -425,15 +434,16 @@
             pltpu.VMEM((2, CP, 8, WIDTH // 2), jnp.bfloat16),
             pltpu.VMEM((ROWS, HEAD), jnp.float32),
             pltpu.VMEM((ROWS, HEAD), jnp.float32),
-            dma((5,)), dma((1,)), dma((2 * PARTS,)),
+            dma((6,)), dma((1,)), dma((2 * PARTS,)),
             dma((PARTS,)), dma((PARTS, 5)), dma((2,)), dma((2,)),
-            pltpu.SMEM((9,), jnp.int32), pltpu.SemaphoreType.REGULAR((2,)),
+            pltpu.SMEM((9,), jnp.int32), pltpu.SMEM((NBLK,), jnp.int32),
+            pltpu.SemaphoreType.REGULAR((2,)),
         ],
         compiler_params=pltpu.CompilerParams(
             collective_id=0, has_side_effects=True, vmem_limit_bytes=32 * 1024 * 1024
         ),
         name="gather_project",
-    )(bounds, hidden, wq, wk, wv, inverse)
+    )(bounds, owner, hidden, wq, wk, wv, inverse)
 
 
 TILE = SPAN * BLOCK
@@ -603,7 +613,7 @@
 def output_kernel(
     slot_ref, heads_ref, wo_ref, out_ref,
     heads, wo, far, near, far_in, near_in, spread, landed, own_sum,
-    w_sem, z_send, z_recv, a_send, a_recv,
+    w_sem, z_send, z_recv, a_send, a_recv, met,
 ):
     me = lax.axis_index("cp")
     tp = lax.axis_index("tp")
@@ -617,15 +627,18 @@
 
     barrier = pltpu.get_barrier_semaphore()
 
-    def greet(k, carry):
-        pl.semaphore_signal(
-            barrier, inc=1, device_id={"cp": lax.rem(me + k, CP)}, device_id_type=MESH
-        )
-        return carry
-
+    core, ycoord, xcoord = lax.rem(me, 2), lax.rem(me // 2, 4), me // 8
+    partner = me + 1 - 2 * core
+
+    def signal(semaphore, target):
+        pl.semaphore_signal(semaphore, inc=1, device_id={"cp": target}, device_id_type=MESH)
+
+    along_x = [(lax.rem(xcoord + n, 4) * 4 + ycoord) * 2 + core for n in (1, 2, 3)]
+    along_y = [(xcoord * 4 + lax.rem(ycoord + n, 4)) * 2 + core for n in (1, 2, 3)]
     pl.semaphore_signal(barrier, inc=1, device_id={"tp": up}, device_id_type=MESH)
     pl.semaphore_signal(barrier, inc=1, device_id={"tp": down}, device_id_type=MESH)
-    lax.fori_loop(1, CP, greet, 0)
+    for target in (*along_x, *along_y, partner):
+        signal(barrier, target)
 
     turned_row = lax.broadcasted_iota(jnp.int32, (QROWS, QROWS), 0)
     turned_column = lax.broadcasted_iota(jnp.int32, (QROWS, QROWS), 1)
@@ -719,7 +732,7 @@
 
     row = lax.broadcasted_iota(jnp.int32, (ROWS, ROWS), 0)
     column = lax.broadcasted_iota(jnp.int32, (ROWS, ROWS), 1)
-    to_owner = (row == slot_ref[...]).astype(jnp.float32).astype(jnp.bfloat16)
+    to_owner = (row == slot_ref[0:1, :]).astype(jnp.float32).astype(jnp.bfloat16)
     origin = (lax.rem(row, BLOCK) // 4) * 8 + (row // BLOCK) * 4 + lax.rem(row, 4)
     to_place = (column == origin).astype(jnp.float32).astype(jnp.bfloat16)
 
@@ -775,8 +788,10 @@
 
     loads[0].wait()
     make_far(0)
-    pl.semaphore_wait(barrier, CP + 1)
+    pl.semaphore_wait(barrier, 9)
     send_far(0)
+    for target in along_x:
+        signal(met.at[0], target)
     make_far(1)
     send_far(1)
     make_far(2)
@@ -784,6 +799,8 @@
     loads[1].wait()
     loads[2].wait()
     send_near(0)
+    pl.semaphore_wait(met.at[0], 3)
+    signal(met.at[1], partner)
     make_far(3)
     send_far(3)
     send_near(1)
@@ -794,6 +811,7 @@
     for c in range(len(CHUNKS)):
         sum_own(c)
     send_near(3)
+    pl.semaphore_wait(met.at[1], 1)
     finish_sum(0)
     send_near(4)
     finish_sum(1)
@@ -830,7 +848,7 @@
             pltpu.VMEM((CP, PIECES, 8, HEAD), bf16),
             pltpu.VMEM((PIECES, ROWS, HEAD), jnp.float32),
             dma((4,)), dma((1,)), dma((3 * len(CHUNKS),)),
-            dma((len(CHUNKS),)), dma((len(CHUNKS),)),
+            dma((len(CHUNKS),)), dma((len(CHUNKS),)), pltpu.SemaphoreType.REGULAR((2,)),
         ],
         compiler_params=pltpu.CompilerParams(
             collective_id=1, has_side_effects=True, vmem_limit_bytes=40 * 1024 * 1024
@@ -842,16 +860,13 @@
 def local(hidden, query_weight, key_matrix, value_matrix, output_weight, bounds, block_owner):
     inverse = rope_inverse(HEAD)
     inverse = jnp.concatenate([inverse, inverse])[None, :]
-    slots = slots_of(block_owner)
-    slot_rows = (slots[:, None] * PORTION + jnp.arange(PORTION, dtype=jnp.int32)[None, :]).reshape(
-        1, ROWS
-    )
     hidden, query_weight, key_matrix, value_matrix, output_weight = (
         pltpu.with_memory_space_constraint(a, pltpu.HBM)
         for a in (hidden, query_weight, key_matrix, value_matrix, output_weight)
     )
-    keys, values, queries, marks = gather_call(
-        pltpu.with_memory_space_constraint(bounds, pltpu.HBM), hidden, query_weight, key_matrix, value_matrix, inverse
+    keys, values, queries, marks, slot_rows = gather_call(
+        pltpu.with_memory_space_constraint(bounds, pltpu.HBM),
+        pltpu.with_memory_space_constraint(block_owner, pltpu.HBM), hidden, query_weight, key_matrix, value_matrix, inverse
     )
     heads = attend_call(
         bounds,

time: 85.2 us -> 84 us (0.986)
  Pallas kernels: 84.2 us -> 82.9 us
    pallas_call x1, Pallas kernels: 28.2 us -> 27 us  [output_call(): pl.pallas_call(output_kernel, out_shape=jax.ShapeDtypeStruct((ROWS, WIDTH...]
where the time goes in v8:
time: 84 us; the launch traced here: 83.9 us
  Pallas kernels  82.9 us (99%)
    pallas_call x1, Pallas kernels, gather_call(): pl.pallas_call(gather_kernel, out_shape=(kv, kv, jax.ShapeDtypeStruct((CP...  44.8 us
    pallas_call x1, Pallas kernels, output_call(): pl.pallas_call(output_kernel, out_shape=jax.ShapeDtypeStruct((ROWS, WIDTH...  27 us
    pallas_call x1, Pallas kernels, attend_call(): pl.pallas_call(attend_kernel, out_shape=jax.ShapeDtypeStruct((GROUPS, HEA...  11.1 us

profile of v8, /device:TPU:1, one launch (start us, length us, event | category | flops | bytes accessed | tf_op | source)
XLA Modules:
  0.0 83.9 jit_solution(7489500418141842984)
XLA Ops:
  0.0 0.1 maximum_bitcast_fusion.inverse_ref
  0.1 0.0 copy-start
  0.1 44.8 %gather_project.1 = (bf16[4,4,2,256,128]{4,3,2,1,0:T(8,128)(2,1)S(1)}, bf16[4,4,2,256,128]{4,3,2,1,0:T(8,128)(2,1)S(1)}, bf16[32,2,8,512]{3,2,1,0:T(8,128)(2,1)S...) custom-call(s32[9]{0:T(128)} %bounds_ref.1, s32[64]{0:T(128)} %owner_hbm.1, bf16[256,1024]{1,0:T(8,128)(2,1)} %hidden_ref.1, ...), custom_call_target="tpu_custom_call" | custom-call | tf_op jit(solution)/shard_map/gather_project/pallas_call | solution.py:418
  44.9 0.0 copy-done
  44.9 11.1 %attend.1.heads_ref = bf16[8,128,256]{2,1,0:T(8,128)(2,1)S(1)} custom-call(s32[9]{0:T(128)S(1)} %copy-done, bf16[512,512]{1,0:T(8,128)(2,1)S(1)} %bitcast.7, bf16[8192,128]{1,0:T(8,128)(2,1)S(1)} %bitcast.5, bf16[8192,128]{1,0:T(8,128)(2,1)S(1)} %bitcast.6, bf16[8192,128]{1,0:T(8,128)(2,1)S(1)} %get-tuple-element.14.mark_ref), custom_call_target="tpu_custom_call" | custom-call | tf_op jit(solution)/shard_map/attend/pallas_call | solution.py:590
  56.0 27.0 %project_out.1 = bf16[256,1024]{1,0:T(8,128)(2,1)S(1)} custom-call(s32[8,256]{1,0:T(8,128)S(1)} %get-tuple-element.10.slot_ref, bf16[8,128,256]{2,1,0:T(8,128)(2,1)S(1)} %attend.1.heads_ref, bf16[1024,4096]{1,0:T(8,128)(2,1)} %wo_ref.1), custom_call_target="tpu_custom_call" | custom-call | tf_op jit(solution)/shard_map/project_out/pallas_call | solution.py:835
  83.1 0.8 copy.9
  (1 shorter events, 0.0 us)
Async XLA Ops:
  0.1 44.8 %copy-start = (s32[9]{0:T(128)S(1)}, s32[9]{0:T(128)}, u32[]{:S(2)}) copy-start(s32[9]{0:T(128)} %bounds_ref.1) | copy-start | bytes 112

commit v9 on v8

--- a/solution.py
+++ b/solution.py
@@ -390,11 +390,11 @@
     queries(1, 2)
     queries(1, 3)
     s1(3)
-    spread(1)
     s2(3)
     s3(1)
     s1(4)
     s2(4)
+    spread(1)
     s3(2)
     s3(3)
     s4(1)

time: 84 us -> 83.2 us (level)
  Pallas kernels: 82.9 us -> 81.7 us
    pallas_call x1, Pallas kernels: 44.8 us -> 43.8 us  [gather_call(): pl.pallas_call(gather_kernel, out_shape=(kv, kv, jax.ShapeDtypeStruct((CP...]
where the time goes in v9:
time: 83.2 us; the launch traced here: 82.6 us
  Pallas kernels  81.7 us (98%)
    pallas_call x1, Pallas kernels, gather_call(): pl.pallas_call(gather_kernel, out_shape=(kv, kv, jax.ShapeDtypeStruct((CP...  43.8 us
    pallas_call x1, Pallas kernels, output_call(): pl.pallas_call(output_kernel, out_shape=jax.ShapeDtypeStruct((ROWS, WIDTH...  26.7 us
    pallas_call x1, Pallas kernels, attend_call(): pl.pallas_call(attend_kernel, out_shape=jax.ShapeDtypeStruct((GROUPS, HEA...  11.1 us

profile of v9, /device:TPU:1, one launch (start us, length us, event | category | flops | bytes accessed | tf_op | source)
XLA Modules:
  0.0 82.6 jit_solution(16649551694538252518)
XLA Ops:
  0.0 0.1 maximum_bitcast_fusion.inverse_ref
  0.1 0.0 copy-start
  0.1 43.8 %gather_project.1 = (bf16[4,4,2,256,128]{4,3,2,1,0:T(8,128)(2,1)S(1)}, bf16[4,4,2,256,128]{4,3,2,1,0:T(8,128)(2,1)S(1)}, bf16[32,2,8,512]{3,2,1,0:T(8,128)(2,1)S...) custom-call(s32[9]{0:T(128)} %bounds_ref.1, s32[64]{0:T(128)} %owner_hbm.1, bf16[256,1024]{1,0:T(8,128)(2,1)} %hidden_ref.1, ...), custom_call_target="tpu_custom_call" | custom-call | tf_op jit(solution)/shard_map/gather_project/pallas_call | solution.py:418
  43.9 0.0 copy-done
  44.0 11.1 %attend.1.heads_ref = bf16[8,128,256]{2,1,0:T(8,128)(2,1)S(1)} custom-call(s32[9]{0:T(128)S(1)} %copy-done, bf16[512,512]{1,0:T(8,128)(2,1)S(1)} %bitcast.7, bf16[8192,128]{1,0:T(8,128)(2,1)S(1)} %bitcast.5, bf16[8192,128]{1,0:T(8,128)(2,1)S(1)} %bitcast.6, bf16[8192,128]{1,0:T(8,128)(2,1)S(1)} %get-tuple-element.14.mark_ref), custom_call_target="tpu_custom_call" | custom-call | tf_op jit(solution)/shard_map/attend/pallas_call | solution.py:590
  55.1 26.7 %project_out.1 = bf16[256,1024]{1,0:T(8,128)(2,1)S(1)} custom-call(s32[8,256]{1,0:T(8,128)S(1)} %get-tuple-element.10.slot_ref, bf16[8,128,256]{2,1,0:T(8,128)(2,1)S(1)} %attend.1.heads_ref, bf16[1024,4096]{1,0:T(8,128)(2,1)} %wo_ref.1), custom_call_target="tpu_custom_call" | custom-call | tf_op jit(solution)/shard_map/project_out/pallas_call | solution.py:835
  81.8 0.8 copy.9
  (1 shorter events, 0.0 us)
Async XLA Ops:
  0.1 43.8 %copy-start = (s32[9]{0:T(128)S(1)}, s32[9]{0:T(128)}, u32[]{:S(2)}) copy-start(s32[9]{0:T(128)} %bounds_ref.1) | copy-start | bytes 112

commit v10 on v9

--- a/solution.py
+++ b/solution.py
@@ -394,8 +394,8 @@
     s3(1)
     s1(4)
     s2(4)
+    s3(2)
     spread(1)
-    s3(2)
     s3(3)
     s4(1)
     s3(4)

time: 83.2 us -> 84.2 us (1.012); the launches traced: 82.6 us -> 84.5 us
  Pallas kernels: 81.7 us -> 83.6 us
    pallas_call x1, Pallas kernels: 11.1 us -> 12.9 us  [attend_call(): pl.pallas_call(attend_kernel, out_shape=jax.ShapeDtypeStruct((GROUPS, HEA...]
where the time goes in v10:
time: 84.2 us; the launch traced here: 84.5 us
  Pallas kernels  83.6 us (99%)
    pallas_call x1, Pallas kernels, gather_call(): pl.pallas_call(gather_kernel, out_shape=(kv, kv, jax.ShapeDtypeStruct((CP...  43.9 us
    pallas_call x1, Pallas kernels, output_call(): pl.pallas_call(output_kernel, out_shape=jax.ShapeDtypeStruct((ROWS, WIDTH...  26.8 us
    pallas_call x1, Pallas kernels, attend_call(): pl.pallas_call(attend_kernel, out_shape=jax.ShapeDtypeStruct((GROUPS, HEA...  12.9 us

profile of v10, /device:TPU:1, one launch (start us, length us, event | category | flops | bytes accessed | tf_op | source)
XLA Modules:
  0.0 84.5 jit_solution(1440250547374629483)
XLA Ops:
  0.0 0.1 maximum_bitcast_fusion.inverse_ref
  0.1 0.0 copy-start
  0.1 43.9 %gather_project.1 = (bf16[4,4,2,256,128]{4,3,2,1,0:T(8,128)(2,1)S(1)}, bf16[4,4,2,256,128]{4,3,2,1,0:T(8,128)(2,1)S(1)}, bf16[32,2,8,512]{3,2,1,0:T(8,128)(2,1)S...) custom-call(s32[9]{0:T(128)} %bounds_ref.1, s32[64]{0:T(128)} %owner_hbm.1, bf16[256,1024]{1,0:T(8,128)(2,1)} %hidden_ref.1, ...), custom_call_target="tpu_custom_call" | custom-call | tf_op jit(solution)/shard_map/gather_project/pallas_call | solution.py:418
  44.0 0.0 copy-done
  44.0 12.9 %attend.1.heads_ref = bf16[8,128,256]{2,1,0:T(8,128)(2,1)S(1)} custom-call(s32[9]{0:T(128)S(1)} %copy-done, bf16[512,512]{1,0:T(8,128)(2,1)S(1)} %bitcast.7, bf16[8192,128]{1,0:T(8,128)(2,1)S(1)} %bitcast.5, bf16[8192,128]{1,0:T(8,128)(2,1)S(1)} %bitcast.6, bf16[8192,128]{1,0:T(8,128)(2,1)S(1)} %get-tuple-element.14.mark_ref), custom_call_target="tpu_custom_call" | custom-call | tf_op jit(solution)/shard_map/attend/pallas_call | solution.py:590
  56.9 26.8 %project_out.1 = bf16[256,1024]{1,0:T(8,128)(2,1)S(1)} custom-call(s32[8,256]{1,0:T(8,128)S(1)} %get-tuple-element.10.slot_ref, bf16[8,128,256]{2,1,0:T(8,128)(2,1)S(1)} %attend.1.heads_ref, bf16[1024,4096]{1,0:T(8,128)(2,1)} %wo_ref.1), custom_call_target="tpu_custom_call" | custom-call | tf_op jit(solution)/shard_map/project_out/pallas_call | solution.py:835
  83.7 0.8 copy.9
  (1 shorter events, 0.0 us)
Async XLA Ops:
  0.1 43.9 %copy-start = (s32[9]{0:T(128)S(1)}, s32[9]{0:T(128)}, u32[]{:S(2)}) copy-start(s32[9]{0:T(128)} %bounds_ref.1) | copy-start | bytes 112

commit v11 on v9

--- a/solution.py
+++ b/solution.py
@@ -376,8 +376,8 @@
     queries(0, 3)
     s0(2)
     s1(1)
+    relay_z(4)
     spread(0)
-    relay_z(4)
     s0(3)
     s3(0)
     s1(2)

time: 83.2 us -> 84.8 us (1.019)
  Pallas kernels: 81.7 us -> 83.7 us
    pallas_call x1, Pallas kernels: 11.1 us -> 12.9 us  [attend_call(): pl.pallas_call(attend_kernel, out_shape=jax.ShapeDtypeStruct((GROUPS, HEA...]
where the time goes in v11:
time: 84.8 us; the launch traced here: 84.7 us
  Pallas kernels  83.7 us (99%)
    pallas_call x1, Pallas kernels, gather_call(): pl.pallas_call(gather_kernel, out_shape=(kv, kv, jax.ShapeDtypeStruct((CP...  43.7 us
    pallas_call x1, Pallas kernels, output_call(): pl.pallas_call(output_kernel, out_shape=jax.ShapeDtypeStruct((ROWS, WIDTH...  27.2 us
    pallas_call x1, Pallas kernels, attend_call(): pl.pallas_call(attend_kernel, out_shape=jax.ShapeDtypeStruct((GROUPS, HEA...  12.9 us

profile of v11, /device:TPU:1, one launch (start us, length us, event | category | flops | bytes accessed | tf_op | source)
XLA Modules:
  0.0 84.7 jit_solution(15064168717105449457)
XLA Ops:
  0.0 0.1 maximum_bitcast_fusion.inverse_ref
  0.1 0.0 copy-start
  0.1 43.7 %gather_project.1 = (bf16[4,4,2,256,128]{4,3,2,1,0:T(8,128)(2,1)S(1)}, bf16[4,4,2,256,128]{4,3,2,1,0:T(8,128)(2,1)S(1)}, bf16[32,2,8,512]{3,2,1,0:T(8,128)(2,1)S...) custom-call(s32[9]{0:T(128)} %bounds_ref.1, s32[64]{0:T(128)} %owner_hbm.1, bf16[256,1024]{1,0:T(8,128)(2,1)} %hidden_ref.1, ...), custom_call_target="tpu_custom_call" | custom-call | tf_op jit(solution)/shard_map/gather_project/pallas_call | solution.py:418
  43.8 0.0 copy-done
  43.8 12.9 %attend.1.heads_ref = bf16[8,128,256]{2,1,0:T(8,128)(2,1)S(1)} custom-call(s32[9]{0:T(128)S(1)} %copy-done, bf16[512,512]{1,0:T(8,128)(2,1)S(1)} %bitcast.7, bf16[8192,128]{1,0:T(8,128)(2,1)S(1)} %bitcast.5, bf16[8192,128]{1,0:T(8,128)(2,1)S(1)} %bitcast.6, bf16[8192,128]{1,0:T(8,128)(2,1)S(1)} %get-tuple-element.14.mark_ref), custom_call_target="tpu_custom_call" | custom-call | tf_op jit(solution)/shard_map/attend/pallas_call | solution.py:590
  56.7 27.2 %project_out.1 = bf16[256,1024]{1,0:T(8,128)(2,1)S(1)} custom-call(s32[8,256]{1,0:T(8,128)S(1)} %get-tuple-element.10.slot_ref, bf16[8,128,256]{2,1,0:T(8,128)(2,1)S(1)} %attend.1.heads_ref, bf16[1024,4096]{1,0:T(8,128)(2,1)} %wo_ref.1), custom_call_target="tpu_custom_call" | custom-call | tf_op jit(solution)/shard_map/project_out/pallas_call | solution.py:835
  83.9 0.8 copy.9
  (1 shorter events, 0.0 us)
Async XLA Ops:
  0.1 43.7 %copy-start = (s32[9]{0:T(128)S(1)}, s32[9]{0:T(128)}, u32[]{:S(2)}) copy-start(s32[9]{0:T(128)} %bounds_ref.1) | copy-start | bytes 112
